TPU v7x, 8 devices: a whole 2x2x1 slice. The times are simulated.
8 devices in a mesh: stage: 2 (over z, y), expert: 4 (over x, core).
Axes of the slice: x: 2, y: 2, z: 1, core: 2. Of those that a mesh axis runs over, the one named last changes fastest.
Arguments:
- x_act: bfloat16 [2, 8192, 512], P('stage', 'expert')
- route_idx: int32 [2, 8192, 8], P('stage', 'expert')
- route_wts: float32 [2, 8192, 8], P('stage', 'expert')
- w_one: bfloat16 [2, 128, 512, 768], P('stage', 'expert')
- w_three: bfloat16 [2, 128, 512, 768], P('stage', 'expert')
- w_two: bfloat16 [2, 128, 768, 512], P('stage', 'expert')
- dy_act: bfloat16 [2, 8192, 512], P('stage', 'expert')
Outputs:
- output 1: bfloat16 [2, 8192, 512], P('stage', 'expert')
- output 2: bfloat16 [2, 8192, 512], P('stage', 'expert')
- output 3: bfloat16 [2, 128, 512, 768], P('stage', 'expert')
- output 4: bfloat16 [2, 128, 512, 768], P('stage', 'expert')
- output 5: bfloat16 [2, 128, 768, 512], P('stage', 'expert')
All inputs are finite; a program needn't handle non-finite values.
Results may differ from a plain program's by a relative error of at most 0.0149914.
Values are sent between devices in bfloat16 or wider.
A program may use at most 1 GiB of HBM per device.

v0:
```python
import jax
import jax.numpy as jnp
from jax import lax
from jax.sharding import PartitionSpec as P


def slot_tables(idx_blk, first_exp, n_exp, capacity):
    n_slot = idx_blk.shape[0] * idx_blk.shape[1]
    slot_ids = idx_blk.reshape(n_slot) - first_exp
    hit_mat = (slot_ids[:, None] == jnp.arange(n_exp, dtype=jnp.int32)[None, :]).astype(jnp.int32)
    slot_rank = jnp.sum(jnp.cumsum(hit_mat, axis=0) * hit_mat, axis=1) - 1
    is_local = (slot_ids >= 0) & (slot_ids < n_exp)
    buf_pos = jnp.where(is_local, slot_ids * capacity + slot_rank, n_exp * capacity)
    slot_at = jnp.full((n_exp * capacity,), n_slot, jnp.int32).at[buf_pos].set(jnp.arange(n_slot, dtype=jnp.int32), mode='drop')
    return buf_pos, slot_at


def take_rows(row_table, row_ids):
    return jnp.take(row_table, row_ids, axis=0, mode='fill', fill_value=0)


def expert_forward(x_buf, w_in_one, w_in_three, w_out):
    pre_one = jnp.einsum('pecd,edf->pecf', x_buf, w_in_one, preferred_element_type=jnp.float32)
    pre_three = jnp.einsum('pecd,edf->pecf', x_buf, w_in_three, preferred_element_type=jnp.float32)
    hidden = (pre_one * jax.nn.sigmoid(pre_one) * pre_three).astype(jnp.bfloat16)
    return jnp.einsum('pecf,efd->pecd', hidden, w_out, preferred_element_type=jnp.float32).astype(jnp.bfloat16)


def expert_backward(x_buf, d_buf, w_in_one, w_in_three, w_out):
    pre_one = jnp.einsum('pecd,edf->pecf', x_buf, w_in_one, preferred_element_type=jnp.float32)
    pre_three = jnp.einsum('pecd,edf->pecf', x_buf, w_in_three, preferred_element_type=jnp.float32)
    sig_one = jax.nn.sigmoid(pre_one)
    act_one = pre_one * sig_one
    hidden = (act_one * pre_three).astype(jnp.bfloat16)
    d_hidden = jnp.einsum('pecd,efd->pecf', d_buf, w_out, preferred_element_type=jnp.float32).astype(jnp.bfloat16).astype(jnp.float32)
    d_three = (d_hidden * act_one).astype(jnp.bfloat16)
    d_one = (d_hidden * pre_three * sig_one * (1.0 + pre_one * (1.0 - sig_one))).astype(jnp.bfloat16)
    dx_buf = (jnp.einsum('pecf,edf->pecd', d_one, w_in_one, preferred_element_type=jnp.float32) + jnp.einsum('pecf,edf->pecd', d_three, w_in_three, preferred_element_type=jnp.float32)).astype(jnp.bfloat16)
    g_one = jnp.einsum('pecd,pecf->edf', x_buf, d_one, preferred_element_type=jnp.float32).astype(jnp.bfloat16)
    g_three = jnp.einsum('pecd,pecf->edf', x_buf, d_three, preferred_element_type=jnp.float32).astype(jnp.bfloat16)
    g_two = jnp.einsum('pecf,pecd->efd', hidden, d_buf, preferred_element_type=jnp.float32).astype(jnp.bfloat16)
    return dx_buf, g_one, g_three, g_two


def solution(mesh):
    n_stage = mesh.shape['stage']
    n_dev = mesh.shape['expert']
    to_next = [(stage_idx, (stage_idx + 1) % n_stage) for stage_idx in range(n_stage)]
    to_prev = [((stage_idx + 1) % n_stage, stage_idx) for stage_idx in range(n_stage)]
    tok_spec = P('stage', 'expert', None)
    w_spec = P('stage', 'expert', None, None)

    def moe_layer(x_act, route_idx, route_wts, w_one, w_three, w_two, dy_act):
        x_src = x_act[0]
        n_tok, model_dim = x_src.shape
        top_k = route_idx.shape[2]
        n_local = w_one.shape[1]
        n_exp = n_local * n_dev
        capacity = 2 * n_tok * top_k // n_exp - 1
        w_in_one, w_in_three, w_out = w_one[0], w_three[0], w_two[0]

        x_dst = lax.ppermute(x_src, 'stage', to_next)
        idx_dst = lax.ppermute(route_idx[0], 'stage', to_next)
        wts_dst = lax.ppermute(route_wts[0], 'stage', to_next)
        buf_pos, slot_at = slot_tables(idx_dst, 0, n_exp, capacity)

        def dispatch(row_src, row_ids):
            send_buf = take_rows(row_src, row_ids).reshape(n_dev, n_local, capacity, model_dim)
            return lax.all_to_all(send_buf, 'expert', 0, 0)

        def combine(buf_rows):
            back_buf = lax.all_to_all(buf_rows, 'expert', 0, 0).reshape(n_exp * capacity, model_dim)
            return take_rows(back_buf, buf_pos).reshape(n_tok, top_k, model_dim)

        out_slot = combine(expert_forward(dispatch(x_dst, slot_at // top_k), w_in_one, w_in_three, w_out))
        y_dst = jnp.sum(wts_dst[:, :, None] * out_slot.astype(jnp.float32), axis=1).astype(jnp.bfloat16)

        x_again, y_dst = lax.optimization_barrier((x_src, y_dst))
        x_dst = lax.ppermute(x_again, 'stage', to_next)
        d_slot = (wts_dst[:, :, None] * dy_act[0][:, None, :].astype(jnp.float32)).astype(jnp.bfloat16).reshape(n_tok * top_k, model_dim)
        dx_buf, g_one, g_three, g_two = expert_backward(dispatch(x_dst, slot_at // top_k), dispatch(d_slot, slot_at), w_in_one, w_in_three, w_out)
        dx_slot = combine(dx_buf)
        dx_dst = jnp.sum(dx_slot.astype(jnp.float32), axis=1).astype(jnp.bfloat16)
        dx_src = lax.ppermute(dx_dst, 'stage', to_prev)
        return y_dst[None], dx_src[None], g_one[None], g_three[None], g_two[None]

    return jax.shard_map(moe_layer, mesh=mesh, in_specs=(tok_spec, tok_spec, tok_spec, w_spec, w_spec, w_spec, tok_spec), out_specs=(tok_spec, tok_spec, w_spec, w_spec, w_spec), check_vma=False)
```

profile of v0, /device:TPU:0, one launch (start us, length us, event | category | flops | bytes accessed | tf_op | source)
XLA Modules:
  0.0 3606.4 jit_solution(4096558719005789420)
XLA Ops:
  41.4 60.4 %scatter_custom_fusion = s32[32640]{0:T(1024)S(1)} fusion(s32[16384]{0:T(1024)S(1)} %bitcast.182, s32[16384]{0:T(1024)S(1)} %iota.11, s32[]{:T(128)} %constant.44.clone.1), kind=kCustom, calls=%fused_computation.92 | custom fusion | bytes 130564 | tf_op jit(solution)/shard_map/scatter | solution.py:14
  102.6 90.7 %gather_fusion.1 = bf16[32640,512]{1,0:T(8,128)(2,1)} fusion(bf16[2048,512]{1,0:T(8,128)(2,1)S(1)} %collective-permute-done.1, s32[32768]{0:T(1024)S(1)} %pad_clamp_fusion.1), kind=kCustom, calls=%fused_computation.clone | custom fusion | bytes 66977280 | tf_op jit(solution)/shard_map/jit(_take)/gather | solution.py:19
  278.0 379.3 %all_to_all.25 = bf16[4,32,255,512]{3,1,2,0:T(8,128)(2,1)} all-to-all(bf16[4,32,255,512]{3,1,2,0:T(8,128)(2,1)} %copy.46), channel_id=1, replica_groups=mesh['stage'=2,'expert'=4] {'expert'}, dimensions={0} | all-to-all | bytes 66846720 | tf_op jit(solution)/shard_map/all_to_all | solution.py:69
  657.3 69.9 %fusion.23 = f32[32,4,255,768]{3,2,1,0:T(8,128)} fusion(bf16[4,32,255,512]{3,1,2,0:T(8,128)(2,1)} %all_to_all.25, bf16[1,32,512,768]{3,2,1,0:T(8,128)(2,1)} %param.15), kind=kOutput, calls=%fused_computation.46 | convolution fusion | flops 25669140480 | bytes 158859264 | tf_op jit(solution)/shard_map/pecd,edf->pecf/dot_general | solution.py:24
  727.2 104.5 %convert_bitcast_fusion = bf16[4,32,255,512]{3,2,0,1:T(8,128)(2,1)} fusion(bf16[1,32,768,512]{3,2,1,0:T(8,128)(2,1)} %param.16, f32[32,4,255,768]{3,2,1,0:T(8,128)} %fusion.23, bf16[4,32,255,512]{3,1,2,0:T(8,128)(2,1)} %all_to_all.25, bf16[1,32,512,768]{3,2,1,0:T(8,128)(2,1)} %param.14), kind=kOutput, calls=%fused_computation.39 | convolution fusion | flops 51505397760 | bytes 217448448 | tf_op jit(solution)/shard_map/pecf,efd->pecd/dot_general | solution.py:26
  831.7 31.3 copy.49
  878.9 355.4 %all-to-all-done.1 = bf16[4,32,255,512]{3,1,2,0:T(8,128)(2,1)} async-done(((bf16[4,32,255,512]{3,1,2,0:T(8,128)(2,1)}), bf16[4,32,255,512]{3,1,2,0:T(8,128)(2,1)}, u32[]{:S(2)}, u32[]{:S(2)}) %all-to-all-start.1) | async-done | bytes 33423392 | tf_op jit(solution)/shard_map/all_to_all | solution.py:72
  1287.3 266.5 %gather_fusion.2 = bf16[16384,512]{1,0:T(8,128)(2,1)} fusion(bf16[32640,512]{1,0:T(8,128)(2,1)} %reshape.145, s32[16384]{0:T(1024)S(1)} %copy-done.10), kind=kCustom, calls=%fused_computation.1.clone | custom fusion | bytes 33619968 | tf_op jit(solution)/shard_map/jit(_take)/gather | solution.py:19
  1584.3 45.3 %collective-permute-done.3 = bf16[2048,512]{1,0:T(8,128)(2,1)S(1)} collective-permute-done((bf16[2048,512]{1,0:T(8,128)(2,1)}, bf16[2048,512]{1,0:T(8,128)(2,1)S(1)}, u32[]{:S(2)}, u32[]{:S(2)}) %collective-permute-start.3) | collective-permute-done | bytes 2097184 | tf_op jit(solution)/shard_map/ppermute | solution.py:79
  1629.6 90.7 %gather_fusion.3 = bf16[32640,512]{1,0:T(8,128)(2,1)} fusion(bf16[2048,512]{1,0:T(8,128)(2,1)S(1)} %collective-permute-done.3, s32[32768]{0:T(1024)S(1)} %copy-done.5), kind=kCustom, calls=%fused_computation.2.clone | custom fusion | bytes 66977280 | tf_op jit(solution)/shard_map/jit(_take)/gather | solution.py:19
  1828.4 100.1 %gather_fusion = bf16[32640,512]{1,0:T(8,128)(2,1)} fusion(bf16[16384,512]{1,0:T(8,128)(2,1)} %fusion.19, s32[32768]{0:T(1024)S(1)} %pad_clamp_fusion), kind=kCustom, calls=%fused_computation.4 | custom fusion | bytes 66977280 | tf_op jit(solution)/shard_map/jit(_take)/gather | solution.py:19
  2012.7 163.6 %all-to-all-done.3 = bf16[4,32,255,512]{3,1,2,0:T(8,128)(2,1)} async-done(((bf16[4,32,255,512]{3,1,2,0:T(8,128)(2,1)}), bf16[4,32,255,512]{3,1,2,0:T(8,128)(2,1)}, u32[]{:S(2)}, u32[]{:S(2)}) %all-to-all-start.3) | async-done | bytes 33423392 | tf_op jit(solution)/shard_map/all_to_all | solution.py:69
  2186.0 51.8 %copy.59 = bf16[4,32,255,512]{2,3,0,1:T(8,128)(2,1)} copy(bf16[4,32,255,512]{3,1,2,0:T(8,128)(2,1)} %all-to-all-done.3) | data formatting | bytes 66846720 | tf_op jit(solution)/shard_map/all_to_all | solution.py:69
  2237.8 60.7 %fusion.39 = f32[32,4,255,768]{3,2,1,0:T(8,128)} fusion(bf16[4,32,255,512]{2,3,0,1:T(8,128)(2,1)} %copy.59, bf16[1,32,512,768]{3,2,1,0:T(8,128)(2,1)} %param.14), kind=kOutput, calls=%fused_computation.56 | convolution fusion | flops 25669140480 | bytes 158859264 | tf_op jit(solution)/shard_map/pecd,edf->pecf/dot_general | solution.py:30
  2298.5 60.7 %fusion.45 = f32[32,4,255,768]{3,2,1,0:T(8,128)} fusion(bf16[4,32,255,512]{2,3,0,1:T(8,128)(2,1)} %copy.59, bf16[1,32,512,768]{3,2,1,0:T(8,128)(2,1)} %param.15), kind=kOutput, calls=%fused_computation.61 | convolution fusion | flops 25669140480 | bytes 158859264 | tf_op jit(solution)/shard_map/pecd,edf->pecf/dot_general | solution.py:31
  2359.2 187.9 %all-to-all-done.2 = bf16[4,32,255,512]{3,1,2,0:T(8,128)(2,1)} async-done(((bf16[4,32,255,512]{3,1,2,0:T(8,128)(2,1)}), bf16[4,32,255,512]{3,1,2,0:T(8,128)(2,1)}, u32[]{:S(2)}, u32[]{:S(2)}) %all-to-all-start.2) | async-done | bytes 33423392 | tf_op jit(solution)/shard_map/all_to_all | solution.py:69
  2547.1 144.0 %fusion.8 = (bf16[4,32,255,768]{3,2,0,1:T(8,128)(2,1)}, bf16[4,32,255,768]{3,2,0,1:T(8,128)(2,1)}) fusion(f32[32,4,255,768]{3,2,1,0:T(8,128)} %fusion.39, f32[32,4,255,768]{3,2,1,0:T(8,128)} %fusion.45, bf16[1,32,768,512]{3,2,1,0:T(8,128)(2,1)} %param.16, bf16[4,32,255,512]{3,1,2,0:T(8,128)(2,1)} %all-to-all-done.2), kind=kOutput, calls=%fused_computation.20 | convolution fusion | flops 26045153280 | bytes 359399424 | tf_op jit(solution)/shard_map/pecd,efd->pecf/dot_general | solution.py:35
  2691.1 60.8 %fusion.37 = f32[32,4,255,512]{3,2,1,0:T(8,128)} fusion(bf16[4,32,255,768]{3,2,0,1:T(8,128)(2,1)} %get-tuple-element.14, bf16[1,32,512,768]{3,2,1,0:T(8,128)(2,1)} %param.14), kind=kOutput, calls=%fused_computation.54 | convolution fusion | flops 25669140480 | bytes 142147584 | tf_op jit(solution)/shard_map/pecf,edf->pecd/dot_general | solution.py:38
  2751.9 57.2 %fusion.17 = bf16[4,32,255,512]{3,2,0,1:T(8,128)(2,1)} fusion(f32[32,4,255,512]{3,2,1,0:T(8,128)} %fusion.37, bf16[4,32,255,768]{3,2,0,1:T(8,128)(2,1)} %get-tuple-element.13, bf16[1,32,512,768]{3,2,1,0:T(8,128)(2,1)} %param.15), kind=kOutput, calls=%fused_computation.34 | convolution fusion | flops 25702563840 | bytes 175570944 | tf_op jit(solution)/shard_map/pecf,edf->pecd/dot_general | solution.py:38
  2850.2 52.4 %fusion.35 = bf16[1,32,512,768]{3,2,1,0:T(8,128)(2,1)} fusion(bf16[4,32,255,512]{2,3,0,1:T(8,128)(2,1)} %copy.59, bf16[4,32,255,768]{3,2,0,1:T(8,128)(2,1)} %get-tuple-element.13), kind=kOutput, calls=%fused_computation.52 | convolution fusion | flops 25681723392 | bytes 108724224 | tf_op jit(solution)/shard_map/pecd,pecf->edf/dot_general | solution.py:40
  2902.6 93.4 %fusion.36 = bf16[1,32,768,512]{3,2,1,0:T(8,128)(2,1)} fusion(bf16[4,32,255,512]{3,1,2,0:T(8,128)(2,1)} %all-to-all-done.2, f32[32,4,255,768]{3,2,1,0:T(8,128)} %fusion.45, f32[32,4,255,768]{3,2,1,0:T(8,128)} %fusion.39), kind=kOutput, calls=%fused_computation.53 | convolution fusion | flops 25832128512 | bytes 259129344 | tf_op jit(solution)/shard_map/pecf,pecd->efd/dot_general | solution.py:41
  2995.9 215.3 %all-to-all-done.4 = bf16[4,32,255,512]{3,1,2,0:T(8,128)(2,1)} async-done(((bf16[4,32,255,512]{3,1,2,0:T(8,128)(2,1)}), bf16[4,32,255,512]{3,1,2,0:T(8,128)(2,1)}, u32[]{:S(2)}, u32[]{:S(2)}) %all-to-all-start.4) | async-done | bytes 33423392 | tf_op jit(solution)/shard_map/all_to_all | solution.py:72
  3264.3 266.4 %gather_fusion.4 = bf16[16384,512]{1,0:T(8,128)(2,1)} fusion(bf16[32640,512]{1,0:T(8,128)(2,1)} %reshape.147, s32[16384]{0:T(1024)S(1)} %copy-done.11), kind=kCustom, calls=%fused_computation.3.clone | custom fusion | bytes 33619968 | tf_op jit(solution)/shard_map/jit(_take)/gather | solution.py:19
  3552.4 52.5 %fusion.34 = bf16[1,32,512,768]{3,2,1,0:T(8,128)(2,1)} fusion(bf16[4,32,255,512]{2,3,0,1:T(8,128)(2,1)} %copy.59, bf16[4,32,255,768]{3,2,0,1:T(8,128)(2,1)} %get-tuple-element.14), kind=kOutput, calls=%fused_computation.51 | convolution fusion | flops 25681723392 | bytes 108724224 | tf_op jit(solution)/shard_map/pecd,pecf->edf/dot_general | solution.py:39
  (102 shorter events, 544.7 us)
Async XLA Ops:
  0.6 5.9 collective-permute-start.2
  4.0 98.6 %collective-permute-start.1 = (bf16[2048,512]{1,0:T(8,128)(2,1)}, bf16[2048,512]{1,0:T(8,128)(2,1)S(1)}, u32[]{:S(2)}, u32[]{:S(2)}) collective-permute-start(bf16[2048,512]{1,0:T(8,128)(2,1)} %bitcast.183), channel_id=1, source_target_pairs={{0,4},{4,0},{1,5},{5,1},{2,6},{6,2},{3,7},{7,3}} | collective-permute-start | bytes 6291464 | tf_op jit(solution)/shard_map/ppermute | solution.py:62
  7.3 186.0 %copy-start.8 = (s32[16384]{0:T(1024)}, s32[16384]{0:T(1024)S(1)}, u32[]{:S(2)}) copy-start(s32[16384]{0:T(1024)S(1)} %eq.25) | copy-start | bytes 196612
  102.5 90.7 %copy-start.14 = (pred[32640]{0:T(1024)(128)(4,1)}, pred[32640]{0:T(1024)(128)(4,1)S(1)}, u32[]{:S(2)}) copy-start(pred[32640]{0:T(1024)(128)(4,1)S(1)} %get-tuple-element.11) | copy-start | bytes 97924
  102.6 90.7 %copy-start.4 = (s32[32768]{0:T(1024)}, s32[32768]{0:T(1024)S(1)}, u32[]{:S(2)}) copy-start(s32[32768]{0:T(1024)S(1)} %pad_clamp_fusion.1) | copy-start | bytes 393220
  862.9 15.9 copy-start.9
  862.9 15.9 copy-start.13
  862.9 371.3 %all-to-all-start.1 = ((bf16[4,32,255,512]{3,1,2,0:T(8,128)(2,1)}), bf16[4,32,255,512]{3,1,2,0:T(8,128)(2,1)}, u32[]{:S(2)}, u32[]{:S(2)}) async-start(bf16[4,32,255,512]{3,1,2,0:T(8,128)(2,1)} %copy.49), calls=%async_computation.1 | async-start | bytes 66846720 | tf_op jit(solution)/shard_map/all_to_all | solution.py:72
  873.2 5.3 collective-permute-start
  878.8 675.0 %copy-start.1 = (f32[2048,8]{1,0:T(8,128)}, f32[2048,8]{1,0:T(8,128)S(1)}, u32[]{:S(2)}) copy-start(f32[2048,8]{1,0:T(8,128)S(1)} %copy.37) | copy-start | bytes 196612
  878.9 674.9 %copy-start.16 = (pred[16384]{0:T(1024)(128)(4,1)}, pred[16384]{0:T(1024)(128)(4,1)S(1)}, u32[]{:S(2)}) copy-start(pred[16384]{0:T(1024)(128)(4,1)S(1)} %compare_and_fusion.2) | copy-start | bytes 49156
  1257.1 30.2 copy-start.10
  1287.3 342.3 %copy-start.5 = (s32[32768]{0:T(1024)S(1)}, s32[32768]{0:T(1024)}, u32[]{:S(2)}) copy-start(s32[32768]{0:T(1024)} %copy-done.4) | copy-start | bytes 393220
  1581.7 138.6 %copy-start.15 = (pred[32640]{0:T(1024)(128)(4,1)S(1)}, pred[32640]{0:T(1024)(128)(4,1)}, u32[]{:S(2)}) copy-start(pred[32640]{0:T(1024)(128)(4,1)} %copy-done.14) | copy-start | bytes 97924
  1581.7 47.9 %collective-permute-start.3 = (bf16[2048,512]{1,0:T(8,128)(2,1)}, bf16[2048,512]{1,0:T(8,128)(2,1)S(1)}, u32[]{:S(2)}, u32[]{:S(2)}) collective-permute-start(bf16[2048,512]{1,0:T(8,128)(2,1)} %bitcast.184), channel_id=1, source_target_pairs={{0,4},{4,0},{1,5},{5,1},{2,6},{6,2},{3,7},{7,3}} | collective-permute-start | bytes 6291464 | tf_op jit(solution)/shard_map/ppermute | solution.py:79
  1805.0 12.8 copy-start.2
  1805.0 13.3 copy-start.18
  1805.1 13.7 copy-start.7
  1805.1 371.2 %all-to-all-start.3 = ((bf16[4,32,255,512]{3,1,2,0:T(8,128)(2,1)}), bf16[4,32,255,512]{3,1,2,0:T(8,128)(2,1)}, u32[]{:S(2)}, u32[]{:S(2)}) async-start(bf16[4,32,255,512]{3,1,2,0:T(8,128)(2,1)} %copy.54), calls=%async_computation.3 | async-start | bytes 66846720 | tf_op jit(solution)/shard_map/all_to_all | solution.py:69
  2176.3 370.8 %all-to-all-start.2 = ((bf16[4,32,255,512]{3,1,2,0:T(8,128)(2,1)}), bf16[4,32,255,512]{3,1,2,0:T(8,128)(2,1)}, u32[]{:S(2)}, u32[]{:S(2)}) async-start(bf16[4,32,255,512]{3,1,2,0:T(8,128)(2,1)} %copy.52), calls=%async_computation.2 | async-start | bytes 66846720 | tf_op jit(solution)/shard_map/all_to_all | solution.py:69
  2840.3 371.0 %all-to-all-start.4 = ((bf16[4,32,255,512]{3,1,2,0:T(8,128)(2,1)}), bf16[4,32,255,512]{3,1,2,0:T(8,128)(2,1)}, u32[]{:S(2)}, u32[]{:S(2)}) async-start(bf16[4,32,255,512]{3,1,2,0:T(8,128)(2,1)} %copy.57), calls=%async_computation.4 | async-start | bytes 66846720 | tf_op jit(solution)/shard_map/all_to_all | solution.py:72
  3234.1 30.2 copy-start.11
  3264.3 266.4 %copy-start.17 = (pred[16384]{0:T(1024)(128)(4,1)S(1)}, pred[16384]{0:T(1024)(128)(4,1)}, u32[]{:S(2)}) copy-start(pred[16384]{0:T(1024)(128)(4,1)} %copy-done.16) | copy-start | bytes 49156
  3550.6 54.3 %collective-permute-start.4 = (bf16[2048,512]{1,0:T(8,128)(2,1)}, bf16[2048,512]{1,0:T(8,128)(2,1)S(1)}, u32[]{:S(2)}, u32[]{:S(2)}) collective-permute-start(bf16[2048,512]{1,0:T(8,128)(2,1)} %bitcast_reduce_fusion), channel_id=1, source_target_pairs={{4,0},{0,4},{5,1},{1,5},{6,2},{2,6},{7,3},{3,7}} | collective-permute-start | bytes 6291464 | tf_op jit(solution)/shard_map/ppermute | solution.py:84
  (5 other events, 25.5 us)
where the time goes:
time: 3630 us; the launch traced here: 3610 us
  local copies, waits for them, and re-layouts  1300 us (36%)
  waiting for transfers between devices  973 us (27%)
  matrix products  756 us (21%)
  blocking collectives  379 us (10%)
  other arithmetic  149 us (4%)
  starting transfers between devices  50.4 us (1%)
    gather x6, local copies, waits for them, and re-layouts, take_rows(): return jnp.take(row_table, row_ids, axis=0, mode='fill', fill_value=0)  845 us
    all_to_all x2, waiting for transfers between devices, combine(): lax.all_to_all(buf_rows, 'expert', 0, 0)  571 us
    all_to_all x1, blocking collectives, dispatch(): return lax.all_to_all(send_buf, 'expert', 0, 0)  379 us
    all_to_all x2, waiting for transfers between devices, dispatch(): return lax.all_to_all(send_buf, 'expert', 0, 0)  351 us
    dot_general x1, matrix products, expert_backward(): jnp.einsum('pecd,efd->pecf', d_buf, w_out, preferred_element_type=jnp.flo...  144 us
    reshape x4, local copies, waits for them, and re-layouts, dispatch(): take_rows(row_src, row_ids).reshape(n_dev, n_local, capacity, model_dim)  123 us
    dot_general x1, matrix products, expert_forward(): jnp.einsum('pecf,efd->pecd', hidden, w_out, preferred_element_type=jnp.fl...  104 us
    dot_general x1, matrix products, expert_backward(): jnp.einsum('pecf,pecd->efd', hidden, d_buf, preferred_element_type=jnp.fl...  93.4 us
  transfers between devices with their start and end apart: 9, of which 7 were waited for; matrix products, arithmetic and copies ran while one was open for 18% of the time, Pallas kernels for 0%

commit v1 on v0

v1 whole, which is shorter than its diff:
```python
import functools

import jax
import jax.numpy as jnp
from jax import lax
from jax.experimental import pallas as pl
from jax.experimental.pallas import tpu as pltpu
from jax.sharding import PartitionSpec as P


F32 = jnp.float32
BF16 = jnp.bfloat16
LIST = 264
PER_SRC = 256
TILE = 256
LANES = 128
STAGE_ROWS = 512
VMEM_LIMIT = 66 * 1000 * 1000


def dot_nn(a, b):
    return lax.dot_general(a, b, (((1,), (0,)), ((), ())), preferred_element_type=F32)


def dot_nt(a, b):
    return lax.dot_general(a, b, (((1,), (1,)), ((), ())), preferred_element_type=F32)


def dot_tn(a, b):
    return lax.dot_general(a, b, (((0,), (0,)), ((), ())), preferred_element_type=F32)


def route_kernel(n_tok, top_k, n_exp, dummy, base_ref, idx_ref, wts_ref, tok_ref, g_ref, cnt_ref):
    base = base_ref[0]

    @pl.loop(0, n_exp)
    def _(e):
        cnt_ref[e] = 0

    @pl.loop(0, n_tok)
    def _(t):
        experts = [idx_ref[t * top_k + j] for j in range(top_k)]
        ranks = [cnt_ref[e] for e in experts]
        wts = [wts_ref[t * top_k + j] for j in range(top_k)]
        for e, r, w in zip(experts, ranks, wts):
            tok_ref[e * LIST + r] = base + t
            g_ref[e * LIST + r] = w
            cnt_ref[e] = r + 1

    @pl.loop(0, n_exp)
    def _(e):
        r = cnt_ref[e]
        for k in range(7):
            tok_ref[e * LIST + r + k] = dummy
            g_ref[e * LIST + r + k] = 0.0
        tok_ref[e * LIST + LIST - 1] = r


def route_lists(idx, wts, base, n_exp, dummy):
    n_tok, top_k = idx.shape
    smem = pl.BlockSpec(memory_space=pltpu.SMEM)
    return pl.pallas_call(
        functools.partial(route_kernel, n_tok, top_k, n_exp, dummy),
        out_shape=(jax.ShapeDtypeStruct((n_exp * LIST,), jnp.int32), jax.ShapeDtypeStruct((n_exp * LIST,), F32)),
        in_specs=[smem, smem, smem],
        out_specs=(smem, smem),
        scratch_shapes=[pltpu.SMEM((n_exp,), jnp.int32)],
        cost_estimate=pl.CostEstimate(flops=60 * 10**8, bytes_accessed=4 * n_exp * LIST * 4, transcendentals=0),
        name='route_lists',
    )(base.reshape(1), idx.reshape(n_tok * top_k), wts.reshape(n_tok * top_k))


def load_table(src_hbm, table, stage, sem, n_rows, n_col):
    n_chunk = n_rows // STAGE_ROWS

    def fetch(i):
        slot = lax.rem(i, 2)
        return pltpu.make_async_copy(src_hbm.at[pl.ds(pl.multiple_of(i * STAGE_ROWS, STAGE_ROWS), STAGE_ROWS)], stage.at[slot], sem.at[slot])

    fetch(0).start()

    @pl.loop(0, n_chunk)
    def _(i):
        @pl.when(i + 1 < n_chunk)
        def _():
            fetch(i + 1).start()

        fetch(i).wait()
        rows = stage[lax.rem(i, 2)]
        for c in range(n_col):
            table[pl.ds(i * (STAGE_ROWS * n_col) + c, STAGE_ROWS, stride=n_col), :] = rows[:, c * LANES:(c + 1) * LANES].astype(F32)

    table[pl.ds(n_rows * n_col, 8), :] = jnp.zeros((8, LANES), F32)


def row_slice(i, n_col):
    return pl.ds(pl.multiple_of(i * n_col, n_col), n_col)


def list_base(p, e, n_local):
    return (p * n_local + e) * LIST


def tile_rows(buf, r0, n_rows, n_col):
    return jnp.concatenate([buf[pl.ds(r0 * n_col + c, n_rows, stride=n_col), :] for c in range(n_col)], axis=1)


def put_rows(buf, r0, rows, n_col):
    for c in range(n_col):
        buf[pl.ds(r0 * n_col + c, rows.shape[0], stride=n_col), :] = rows[:, c * LANES:(c + 1) * LANES]


def for_lists(tok, e, n_src, n_local, step, unroll):
    row = jnp.int32(0)
    for p in range(n_src):
        base = list_base(p, e, n_local)
        cnt = tok[base + LIST - 1]

        def group(i, _, base=base, row=row):
            step(base + i * unroll, row + i * unroll)
            return 0

        lax.fori_loop(0, lax.div(cnt + (unroll - 1), unroll), group, 0)
        row = row + cnt
    return row


def for_tiles(total, tile):
    n_full = lax.div(total + (TILE // 2 - 1), TILE)

    @pl.loop(0, n_full)
    def _(i):
        tile(i * TILE, TILE)

    @pl.when(total > n_full * TILE)
    def _():
        tile(n_full * TILE, TILE // 2)


def add_rows(tok, g, acc, buf, e, n_src, n_local, n_col):
    def step(pos, row):
        toks = [tok[pos + k] for k in range(8)]
        rows = [buf[row_slice(row + k, n_col), :] for k in range(8)]
        if g is not None:
            rows = [r * g[pos + k] for k, r in enumerate(rows)]
        sums = [acc[row_slice(t, n_col), :] + r for t, r in zip(toks, rows)]
        for t, s in zip(toks, sums):
            acc[row_slice(t, n_col), :] = s

    for_lists(tok, e, n_src, n_local, step, 8)


def forward_kernel(n_src, n_local, n_rows, n_col, tok, g, x_hbm, w_one, w_three, w_two, y_hbm, table, acc, buf, stage, sem):
    e = pl.program_id(0)

    @pl.when(e == 0)
    def _():
        acc[...] = jnp.zeros_like(acc)
        buf[...] = jnp.zeros_like(buf)
        load_table(x_hbm, table, stage, sem, n_rows, n_col)

    def pick(pos, row):
        rows = [table[row_slice(tok[pos + k], n_col), :] for k in range(8)]
        for k in range(8):
            buf[row_slice(row + k, n_col), :] = rows[k]

    total = for_lists(tok, e, n_src, n_local, pick, 8)

    def tile(r0, m):
        x = tile_rows(buf, r0, m, n_col).astype(BF16)
        pre_one = dot_nn(x, w_one[0])
        pre_three = dot_nn(x, w_three[0])
        hidden = (pre_one * jax.nn.sigmoid(pre_one) * pre_three).astype(BF16)
        put_rows(buf, r0, dot_nn(hidden, w_two[0]).astype(BF16).astype(F32), n_col)

    for_tiles(total, tile)
    add_rows(tok, g, acc, buf, e, n_src, n_local, n_col)

    @pl.when(e == n_local - 1)
    def _():
        out = pltpu.make_async_copy(acc.at[pl.ds(0, n_rows * n_col)], y_hbm, sem.at[0])
        out.start()
        out.wait()


def buf_rows(n_src):
    return n_src * PER_SRC + 8


def forward_partial(tok, g, x_all, w_one, w_three, w_two):
    n_rows, model = x_all.shape
    n_local, _, ffn = w_one.shape
    n_src = tok.shape[0] // (n_local * LIST)
    n_col = model // LANES
    smem = pl.BlockSpec(memory_space=pltpu.SMEM)
    hbm = pl.BlockSpec(memory_space=pl.ANY)
    per_expert = lambda a, b: pl.BlockSpec((1, a, b), lambda e: (e, 0, 0))
    pairs = n_rows * 8 // n_src
    return pl.pallas_call(
        functools.partial(forward_kernel, n_src, n_local, n_rows, n_col),
        out_shape=jax.ShapeDtypeStruct((n_rows * n_col, LANES), F32),
        grid=(n_local,),
        in_specs=[smem, smem, hbm, per_expert(model, ffn), per_expert(model, ffn), per_expert(ffn, model)],
        out_specs=hbm,
        scratch_shapes=[
            pltpu.VMEM((n_rows * n_col + 8, LANES), F32),
            pltpu.VMEM((n_rows * n_col + 8, LANES), F32),
            pltpu.VMEM((buf_rows(n_src) * n_col, LANES), F32),
            pltpu.VMEM((2, STAGE_ROWS, model), BF16),
            pltpu.SemaphoreType.DMA((2,)),
        ],
        compiler_params=pltpu.CompilerParams(dimension_semantics=('arbitrary',), vmem_limit_bytes=VMEM_LIMIT),
        cost_estimate=pl.CostEstimate(flops=6 * pairs * model * ffn, bytes_accessed=6 * n_local * model * ffn, transcendentals=0),
        name='forward_partial',
    )(tok, g, x_all, w_one, w_three, w_two)


def pick_kernel(n_src, n_local, n_rows, n_col, tok, g, x_hbm, dy_hbm, x_out, d_out, x_table, d_table, x_buf, d_buf, stage, sem):
    e = pl.program_id(0)

    @pl.when(e == 0)
    def _():
        load_table(x_hbm, x_table, stage, sem, n_rows, n_col)
        load_table(dy_hbm, d_table, stage, sem, n_rows, n_col)

    def pick(pos, row):
        toks = [tok[pos + k] for k in range(8)]
        x_rows = [x_table[row_slice(t, n_col), :] for t in toks]
        d_rows = [d_table[row_slice(t, n_col), :] * g[pos + k] for k, t in enumerate(toks)]
        for k in range(8):
            x_buf[row_slice(row + k, n_col), :] = x_rows[k]
            d_buf[row_slice(row + k, n_col), :] = d_rows[k]

    total = for_lists(tok, e, n_src, n_local, pick, 8)

    @pl.loop(0, lax.div(total + (TILE - 1), TILE))
    def _(i):
        r0 = pl.multiple_of(i * TILE, TILE)
        used = lax.broadcasted_iota(jnp.int32, (TILE, n_col * LANES), 0) < total - r0
        x_out[0, pl.ds(r0, TILE), :] = jnp.where(used, tile_rows(x_buf, r0, TILE, n_col), 0.0).astype(BF16)
        d_out[0, pl.ds(r0, TILE), :] = jnp.where(used, tile_rows(d_buf, r0, TILE, n_col), 0.0).astype(BF16)


def pick_rows(tok, g, x_all, dy_all, n_local):
    n_rows, model = x_all.shape
    n_src = tok.shape[0] // (n_local * LIST)
    n_col = model // LANES
    cap = n_src * PER_SRC
    smem = pl.BlockSpec(memory_space=pltpu.SMEM)
    hbm = pl.BlockSpec(memory_space=pl.ANY)
    table = pltpu.VMEM((n_rows * n_col + 8, LANES), F32)
    buf = pltpu.VMEM((buf_rows(n_src) * n_col, LANES), F32)
    rows_out = jax.ShapeDtypeStruct((n_local, cap, model), BF16)
    rows_spec = pl.BlockSpec((1, cap, model), lambda e: (e, 0, 0))
    return pl.pallas_call(
        functools.partial(pick_kernel, n_src, n_local, n_rows, n_col),
        out_shape=(rows_out, rows_out),
        grid=(n_local,),
        in_specs=[smem, smem, hbm, hbm],
        out_specs=(rows_spec, rows_spec),
        scratch_shapes=[table, table, buf, buf, pltpu.VMEM((2, STAGE_ROWS, model), BF16), pltpu.SemaphoreType.DMA((2,))],
        compiler_params=pltpu.CompilerParams(dimension_semantics=('arbitrary',), vmem_limit_bytes=VMEM_LIMIT),
        cost_estimate=pl.CostEstimate(flops=40 * 10**9, bytes_accessed=4 * n_local * cap * model, transcendentals=0),
        name='pick_rows',
    )(tok, g, x_all, dy_all)


def list_total(tok, e, n_src, n_local):
    total = tok[list_base(0, e, n_local) + LIST - 1]
    for p in range(1, n_src):
        total = total + tok[list_base(p, e, n_local) + LIST - 1]
    return total


def backward_kernel(n_src, n_local, n_rows, n_col, tok, x_ref, d_ref, w_one, w_three, w_two, dx_hbm, h_ref, d1_ref, d3_ref, acc, buf, sem):
    e = pl.program_id(0)

    @pl.when(e == 0)
    def _():
        acc[...] = jnp.zeros_like(acc)
        buf[...] = jnp.zeros_like(buf)

    def tile(r0, m):
        rows = pl.ds(pl.multiple_of(r0, TILE // 2), m)
        x = x_ref[0, rows, :]
        pre_one = dot_nn(x, w_one[0])
        pre_three = dot_nn(x, w_three[0])
        d_hidden = dot_nt(d_ref[0, rows, :], w_two[0]).astype(BF16).astype(F32)
        sig_one = jax.nn.sigmoid(pre_one)
        act_one = pre_one * sig_one
        h_ref[0, rows, :] = (act_one * pre_three).astype(BF16)
        d_three = (d_hidden * act_one).astype(BF16)
        d_one = (d_hidden * pre_three * sig_one * (1.0 + pre_one * (1.0 - sig_one))).astype(BF16)
        d1_ref[0, rows, :] = d_one
        d3_ref[0, rows, :] = d_three
        dx = dot_nt(d_one, w_one[0]) + dot_nt(d_three, w_three[0])
        put_rows(buf, r0, dx.astype(BF16).astype(F32), n_col)
        if m < TILE:
            rest = pl.ds(pl.multiple_of(r0 + m, TILE // 2), TILE - m)
            for ref in (h_ref, d1_ref, d3_ref):
                ref[0, rest, :] = jnp.zeros((TILE - m, ref.shape[2]), BF16)

    for_tiles(list_total(tok, e, n_src, n_local), tile)
    add_rows(tok, None, acc, buf, e, n_src, n_local, n_col)

    @pl.when(e == n_local - 1)
    def _():
        out = pltpu.make_async_copy(acc.at[pl.ds(0, n_rows * n_col)], dx_hbm, sem)
        out.start()
        out.wait()


def backward_partial(tok, x_rows, d_rows, w_one, w_three, w_two, n_rows):
    n_local, cap, model = x_rows.shape
    ffn = w_one.shape[2]
    n_src = cap // PER_SRC
    n_col = model // LANES
    smem = pl.BlockSpec(memory_space=pltpu.SMEM)
    hbm = pl.BlockSpec(memory_space=pl.ANY)
    per_expert = lambda a, b: pl.BlockSpec((1, a, b), lambda e: (e, 0, 0))
    ffn_out = jax.ShapeDtypeStruct((n_local, cap, ffn), BF16)
    pairs = n_rows * 8 // n_src
    return pl.pallas_call(
        functools.partial(backward_kernel, n_src, n_local, n_rows, n_col),
        out_shape=(jax.ShapeDtypeStruct((n_rows * n_col, LANES), F32), ffn_out, ffn_out, ffn_out),
        grid=(n_local,),
        in_specs=[smem, per_expert(cap, model), per_expert(cap, model), per_expert(model, ffn), per_expert(model, ffn), per_expert(ffn, model)],
        out_specs=(hbm, per_expert(cap, ffn), per_expert(cap, ffn), per_expert(cap, ffn)),
        scratch_shapes=[
            pltpu.VMEM((n_rows * n_col + 8, LANES), F32),
            pltpu.VMEM((buf_rows(n_src) * n_col, LANES), F32),
            pltpu.SemaphoreType.DMA,
        ],
        compiler_params=pltpu.CompilerParams(dimension_semantics=('arbitrary',), vmem_limit_bytes=VMEM_LIMIT),
        cost_estimate=pl.CostEstimate(flops=10 * pairs * model * ffn, bytes_accessed=6 * n_local * cap * ffn, transcendentals=0),
        name='backward_partial',
    )(tok, x_rows, d_rows, w_one, w_three, w_two)


def grad_kernel(n_src, n_local, tok, x_ref, d_ref, h_ref, d1_ref, d3_ref, g1_ref, g3_ref, g2_ref):
    total = list_total(tok, pl.program_id(0), n_src, n_local)
    used = lax.div(total + (TILE - 1), TILE)
    for n in range(1, n_src * PER_SRC // TILE + 1):
        @pl.when(used == n)
        def _(n=n):
            rows = pl.ds(0, n * TILE)
            g1_ref[0] = dot_tn(x_ref[0, rows, :], d1_ref[0, rows, :]).astype(BF16)
            g3_ref[0] = dot_tn(x_ref[0, rows, :], d3_ref[0, rows, :]).astype(BF16)
            g2_ref[0] = dot_tn(h_ref[0, rows, :], d_ref[0, rows, :]).astype(BF16)


def weight_grads(tok, x_rows, d_rows, hidden, d_one, d_three):
    n_local, cap, model = x_rows.shape
    ffn = hidden.shape[2]
    n_src = cap // PER_SRC
    per_expert = lambda a, b: pl.BlockSpec((1, a, b), lambda e: (e, 0, 0))
    in_grad = jax.ShapeDtypeStruct((n_local, model, ffn), BF16)
    pairs = n_local * cap // 2
    return pl.pallas_call(
        functools.partial(grad_kernel, n_src, n_local),
        out_shape=(in_grad, in_grad, jax.ShapeDtypeStruct((n_local, ffn, model), BF16)),
        grid=(n_local,),
        in_specs=[pl.BlockSpec(memory_space=pltpu.SMEM), per_expert(cap, model), per_expert(cap, model), per_expert(cap, ffn), per_expert(cap, ffn), per_expert(cap, ffn)],
        out_specs=(per_expert(model, ffn), per_expert(model, ffn), per_expert(ffn, model)),
        compiler_params=pltpu.CompilerParams(dimension_semantics=('arbitrary',), vmem_limit_bytes=VMEM_LIMIT),
        cost_estimate=pl.CostEstimate(flops=6 * pairs * model * ffn, bytes_accessed=6 * n_local * cap * ffn, transcendentals=0),
        name='weight_grads',
    )(tok, x_rows, d_rows, hidden, d_one, d_three)


def solution(mesh):
    n_stage = mesh.shape['stage']
    n_dev = mesh.shape['expert']
    to_next = [(stage_idx, (stage_idx + 1) % n_stage) for stage_idx in range(n_stage)]
    to_prev = [((stage_idx + 1) % n_stage, stage_idx) for stage_idx in range(n_stage)]
    tok_spec = P('stage', 'expert', None)
    w_spec = P('stage', 'expert', None, None)

    def moe_body(x_act, route_idx, route_wts, w_one, w_three, w_two, dy_act):
        n_tok, model_dim = x_act.shape[1:]
        n_local = w_one.shape[1]
        n_exp = n_local * n_dev
        n_rows = n_tok * n_dev
        w_in_one, w_in_three, w_out = w_one[0], w_three[0], w_two[0]

        def gather_tokens(rows):
            return lax.all_gather(rows, 'expert', axis=0, tiled=True)

        def scatter_sums(partial):
            own = lax.psum_scatter(partial, 'expert', scatter_dimension=0, tiled=True)
            return own.reshape(n_tok, model_dim).astype(BF16)

        x_dst = lax.ppermute(x_act[0], 'stage', to_next)
        idx_dst = lax.ppermute(route_idx[0], 'stage', to_next)
        wts_dst = lax.ppermute(route_wts[0], 'stage', to_next)
        x_dst, idx_dst, wts_dst, x_again, dy_src = lax.optimization_barrier((x_dst, idx_dst, wts_dst, x_act[0], dy_act[0]))
        x_all = gather_tokens(x_dst)
        x_dst_again = lax.ppermute(x_again, 'stage', to_next)
        tok_own, g_own = route_lists(idx_dst, wts_dst, lax.axis_index('expert') * n_tok, n_exp, n_rows)
        n_list = n_local * LIST
        lists = jnp.concatenate([tok_own.reshape(n_dev, n_list).astype(F32), g_own.reshape(n_dev, n_list)], axis=1)
        lists = lax.all_to_all(lists, 'expert', 0, 0, tiled=True)
        lists, x_dst_again, dy_src, x_all = lax.optimization_barrier((lists, x_dst_again, dy_src, x_all))
        tok = lists[:, :n_list].astype(jnp.int32).reshape(n_dev * n_list)
        g = lists[:, n_list:].reshape(n_dev * n_list)
        dy_all = gather_tokens(dy_src)
        x_all_again = gather_tokens(x_dst_again)

        y_sum = forward_partial(tok, g, x_all, w_in_one, w_in_three, w_out)
        y_sum, x_all_again, dy_all = lax.optimization_barrier((y_sum, x_all_again, dy_all))
        y_dst = scatter_sums(y_sum)

        x_rows, d_rows = pick_rows(tok, g, x_all_again, dy_all, n_local)
        dx_sum, hidden, d_one, d_three = backward_partial(tok, x_rows, d_rows, w_in_one, w_in_three, w_out, n_rows)
        dx_dst = scatter_sums(dx_sum)
        dx_src = lax.ppermute(dx_dst, 'stage', to_prev)
        g_one, g_three, g_two = weight_grads(tok, x_rows, d_rows, hidden, d_one, d_three)
        return y_dst[None], dx_src[None], g_one[None], g_three[None], g_two[None]

    return jax.shard_map(moe_body, mesh=mesh, in_specs=(tok_spec, tok_spec, tok_spec, w_spec, w_spec, w_spec, tok_spec), out_specs=(tok_spec, tok_spec, w_spec, w_spec, w_spec), check_vma=False)
```

time: 3630 us -> 960 us (0.26)
  local copies, waits for them, and re-layouts: 1300 us -> 16.3 us
  matrix products: 756 us -> 0 us
  waiting for transfers between devices: 973 us -> 279 us
  Pallas kernels: 0 us -> 626 us
  blocking collectives: 379 us -> 8.65 us
  other arithmetic: 149 us -> 5.79 us
  starting transfers between devices: 50.4 us -> 8.97 us
    all_to_all x4 -> x0, waiting for transfers between devices: 922 us -> none  [the longest x2 571 us: combine(): lax.all_to_all(buf_rows, 'expert', 0, 0)]
    gather x6 -> x0, local copies, waits for them, and re-layouts: 845 us -> none  [take_rows(): return jnp.take(row_table, row_ids, axis=0, mode='fill', fill_value=0)]
    dot_general x10 -> x0, matrix products: 756 us -> none  [the longest x1 144 us: expert_backward(): jnp.einsum('pecd,efd->pecf', d_buf, w_out, preferred_element_type=jnp.flo...]
    pallas_call x0 -> x5, Pallas kernels: none -> 626 us  [the longest x1 181 us: backward_partial(): pl.pallas_call(functools.partial(backward_kernel, n_src, n_local, n_rows,...]
    all_to_all x1, blocking collectives: 379 us -> 8.65 us  [moe_body(): lists = lax.all_to_all(lists, 'expert', 0, 0, tiled=True)]
    reduce_scatter x0 -> x2, waiting for transfers between devices: none -> 195 us  [scatter_sums(): own = lax.psum_scatter(partial, 'expert', scatter_dimension=0, tiled=True)]
    reshape x6 -> x5, local copies, waits for them, and re-layouts: 183 us -> 4.54 us  [the longest x1 1.08 us: route_lists(): idx.reshape(n_tok * top_k)]
    all_to_all x3 -> x1, local copies, waits for them, and re-layouts: 97.5 us -> 0.19 us  [moe_body(): lists = lax.all_to_all(lists, 'expert', 0, 0, tiled=True)]
  transfers between devices with their start and end apart: 9 -> 10, of which waited for: 7 -> 5; matrix products, arithmetic and copies ran while one was open for 18% -> 2% of each run, Pallas kernels for 0% -> 37%
where the time goes in v1:
time: 960 us; the launch traced here: 959 us
  Pallas kernels  626 us (65%)
  waiting for transfers between devices  279 us (29%)
  local copies, waits for them, and re-layouts  16.3 us (2%)
  between operations  13.9 us (1%)
    reduce_scatter x2, waiting for transfers between devices, scatter_sums(): own = lax.psum_scatter(partial, 'expert', scatter_dimension=0, tiled=True)  195 us
    pallas_call x1, Pallas kernels, backward_partial(): pl.pallas_call(functools.partial(backward_kernel, n_src, n_local, n_rows,...  181 us
    pallas_call x1, Pallas kernels, forward_partial(): pl.pallas_call(functools.partial(forward_kernel, n_src, n_local, n_rows,...  148 us
    pallas_call x1, Pallas kernels, weight_grads(): pl.pallas_call(functools.partial(grad_kernel, n_src, n_local), out_shape=...  113 us
    pallas_call x1, Pallas kernels, route_lists(): pl.pallas_call(functools.partial(route_kernel, n_tok, top_k, n_exp, dummy...  97.8 us
    pallas_call x1, Pallas kernels, pick_rows(): pl.pallas_call(functools.partial(pick_kernel, n_src, n_local, n_rows, n_c...  85.6 us
    ppermute x1, waiting for transfers between devices, moe_body(): idx_dst = lax.ppermute(route_idx[0], 'stage', to_next)  45.9 us
    ppermute x1, waiting for transfers between devices, moe_body(): x_dst_again = lax.ppermute(x_again, 'stage', to_next)  36.3 us
  transfers between devices with their start and end apart: 10, of which 5 were waited for; matrix products, arithmetic and copies ran while one was open for 2% of the time, Pallas kernels for 37%

profile of v1, /device:TPU:0, one launch (start us, length us, event | category | flops | bytes accessed | tf_op | source)
XLA Modules:
  0.0 958.8 jit_solution(12476670525351076190)
XLA Ops:
  7.2 3.4 collective-permute-start
  10.6 2.0 collective-permute-start.2
  12.6 45.9 %collective-permute-done.1 = s32[2048,8]{0,1:T(8,128)S(1)} collective-permute-done((s32[2048,8]{0,1:T(8,128)}, s32[2048,8]{0,1:T(8,128)S(1)}, u32[]{:S(2)}, u32[]{:S(2)}) %collective-permute-start.1) | collective-permute-done | bytes 65568 | tf_op jit(solution)/shard_map/ppermute | solution.py:394
  59.2 1.3 copy-done
  61.0 1.1 reshape.47.idx_ref
  62.4 1.1 reshape.48.wts_ref
  63.5 97.8 %route_lists.1 = (s32[33792]{0:T(1024)}, f32[33792]{0:T(1024)}) custom-call(s32[1]{0:T(128)} %bitcast.base_ref, s32[16384]{0:T(1024)} %reshape.47.idx_ref, f32[16384]{0:T(1024)} %reshape.48.wts_ref), custom_call_target="tpu_custom_call" | custom-call | flops 6000000000 | bytes 540672 | tf_op jit(solution)/shard_map/route_lists/pallas_call | solution.py:62
  162.2 1.0 reshape.49
  163.2 1.8 collective-permute-start.3
  165.2 8.7 all_to_all.12
  173.9 36.3 %collective-permute-done.3 = bf16[2048,512]{1,0:T(8,128)(2,1)S(1)} collective-permute-done((bf16[2048,512]{1,0:T(8,128)(2,1)}, bf16[2048,512]{1,0:T(8,128)(2,1)S(1)}, u32[]{:S(2)}, u32[]{:S(2)}) %collective-permute-start.3) | collective-permute-done | bytes 2097184 | tf_op jit(solution)/shard_map/ppermute | solution.py:398
  210.2 1.3 copy-done.1
  213.8 147.9 %forward_partial.1 = f32[32768,128]{1,0:T(8,128)} custom-call(s32[33792]{0:T(1024)} %reshape.50.tok, f32[33792]{0:T(1024)} %reshape.51.g, bf16[8192,512]{1,0:T(8,128)(2,1)} %all-gather.4.cloned.1.call-done.x_hbm, bf16[32,512,768]{2,1,0:T(8,128)(2,1)} %bitcast.17, bf16[32,512,768]{2,1,0:T(8,128)(2,1)} %bitcast.19, bf16[32,768,512]{2,1,0:T(8,128)(2,1)} %bitcast.21), custom_call_target="tpu_custom_call" | custom-call | flops 38654705664 | bytes 75497472 | tf_op jit(solution)/shard_map/forward_partial/pallas_call | solution.py:199
  361.8 85.6 %pick_rows.1 = (bf16[32,1024,512]{2,1,0:T(8,128)(2,1)}, bf16[32,1024,512]{2,1,0:T(8,128)(2,1)}) custom-call(s32[33792]{0:T(1024)} %reshape.50.tok, f32[33792]{0:T(1024)} %reshape.51.g, bf16[8192,512]{1,0:T(8,128)(2,1)} %all-gather.6.cloned.1.call-done.x_hbm, bf16[8192,512]{1,0:T(8,128)(2,1)} %all-gather.8.cloned.1.call-done.dy_hbm), custom_call_target="tpu_custom_call" | custom-call | flops 40000000000 | bytes 67108864 | tf_op jit(solution)/shard_map/pick_rows/pallas_call | solution.py:255
  447.3 181.1 %backward_partial.1 = (f32[32768,128]{1,0:T(8,128)}, bf16[32,1024,768]{2,1,0:T(8,128)(2,1)}, bf16[32,1024,768]{2,1,0:T(8,128)(2,1)}, bf16[32,1024,768]{2,1,0:T(8,128)(2,1)}) custom-call(s32[33792]{0:T(1024)} %reshape.50.tok, bf16[32,1024,512]{2,1,0:T(8,128)(2,1)} %get-tuple-element.42.x_ref, bf16[32,1024,512]{2,1,0:T(8,128)(2,1)} %get-tuple-element.43.d_ref, ...), custom_call_target="tpu_custom_call" | custom-call | flops 64424509440 | bytes 150994944 | tf_op jit(solution)/shard_map/backward_partial/pallas_call | solution.py:323
  629.0 193.3 %reduce-scatter.5.cloned.1.call-done = f32[8192,128]{1,0:T(8,128)} async-done(((f32[32768,128]{1,0:T(8,128)}), f32[8192,128]{1,0:T(8,128)}) %reduce-scatter.5.cloned.1.call-update) | async-done | bytes 4194320 | tf_op jit(solution)/shard_map/reduce_scatter | solution.py:390
  822.4 2.4 convert_element_type.33
  824.8 2.6 convert_element_type.34
  827.3 1.5 collective-permute-start.4
  828.8 113.5 %weight_grads.1 = (bf16[32,512,768]{2,1,0:T(8,128)(2,1)}, bf16[32,512,768]{2,1,0:T(8,128)(2,1)}, bf16[32,768,512]{2,1,0:T(8,128)(2,1)}) custom-call(s32[33792]{0:T(1024)} %reshape.50.tok, bf16[32,1024,512]{2,1,0:T(8,128)(2,1)} %get-tuple-element.42.x_ref, bf16[32,1024,512]{2,1,0:T(8,128)(2,1)} %get-tuple-element.43.d_ref, ...), custom_call_target="tpu_custom_call" | custom-call | flops 38654705664 | bytes 150994944 | tf_op jit(solution)/shard_map/weight_grads/pallas_call | solution.py:359
  942.2 2.1 reduce-scatter.3.cloned.1.call-done
  944.3 2.4 convert_element_type.31
  946.7 2.6 convert_element_type.32
  949.2 3.0 copy.20
  (29 shorter events, 5.6 us)
Async XLA Ops:
  7.2 203.0 %all-gather.4.cloned.1.call-start = ((), (), s32[]{:S(2)}) async-start(), calls=%async_computation.3 | async-start | bytes 10485760 | tf_op jit(solution)/shard_map/all_gather | solution.py:387
  7.2 52.0 %collective-permute-start = (bf16[2048,512]{1,0:T(8,128)(2,1)}, bf16[2048,512]{1,0:T(8,128)(2,1)S(1)}, u32[]{:S(2)}, u32[]{:S(2)}) collective-permute-start(bf16[2048,512]{1,0:T(8,128)(2,1)} %bitcast.26), channel_id=1, source_target_pairs={{0,4},{4,0},{1,5},{5,1},{2,6},{6,2},{3,7},{7,3}} | collective-permute-start | bytes 6291464 | tf_op jit(solution)/shard_map/ppermute | solution.py:393
  10.6 47.9 %collective-permute-start.1 = (s32[2048,8]{0,1:T(8,128)}, s32[2048,8]{0,1:T(8,128)S(1)}, u32[]{:S(2)}, u32[]{:S(2)}) collective-permute-start(s32[2048,8]{0,1:T(8,128)} %bitcast.28), channel_id=1, source_target_pairs={{0,4},{4,0},{1,5},{5,1},{2,6},{6,2},{3,7},{7,3}} | collective-permute-start | bytes 196616 | tf_op jit(solution)/shard_map/ppermute | solution.py:394
  10.6 48.6 %collective-permute-start.2 = (f32[2048,8]{0,1:T(8,128)}, f32[2048,8]{0,1:T(8,128)S(1)}, u32[]{:S(2)}, u32[]{:S(2)}) collective-permute-start(f32[2048,8]{0,1:T(8,128)} %bitcast.29), channel_id=1, source_target_pairs={{0,4},{4,0},{1,5},{5,1},{2,6},{6,2},{3,7},{7,3}} | collective-permute-start | bytes 196616 | tf_op jit(solution)/shard_map/ppermute | solution.py:395
  59.2 1.3 copy-start
  60.6 301.2 %all-gather.6.cloned.1.call-start = ((), (), s32[]{:S(2)}) async-start(), calls=%async_computation.4 | async-start | bytes 10485760 | tf_op jit(solution)/shard_map/all_gather | solution.py:387
  163.2 47.0 %collective-permute-start.3 = (bf16[2048,512]{1,0:T(8,128)(2,1)}, bf16[2048,512]{1,0:T(8,128)(2,1)S(1)}, u32[]{:S(2)}, u32[]{:S(2)}) collective-permute-start(bf16[2048,512]{1,0:T(8,128)(2,1)} %bitcast.27), channel_id=1, source_target_pairs={{0,4},{4,0},{1,5},{5,1},{2,6},{6,2},{3,7},{7,3}} | collective-permute-start | bytes 6291464 | tf_op jit(solution)/shard_map/ppermute | solution.py:398
  210.2 1.3 copy-start.1
  211.5 150.2 %all-gather.8.cloned.1.call-start = ((), (), s32[]{:S(2)}) async-start(), calls=%async_computation.5 | async-start | bytes 10485760 | tf_op jit(solution)/shard_map/all_gather | solution.py:387
  212.3 610.1 %reduce-scatter.5.cloned.1.call-start = ((), (), s32[]{:S(2)}) async-start(), calls=%async_computation.7 | async-start | bytes 20971520 | tf_op jit(solution)/shard_map/reduce_scatter | solution.py:390
  628.4 315.9 %reduce-scatter.3.cloned.1.call-start = ((), (), s32[]{:S(2)}) async-start(), calls=%async_computation.6 | async-start | bytes 20971520 | tf_op jit(solution)/shard_map/reduce_scatter | solution.py:390
  827.3 121.9 %collective-permute-start.4 = (bf16[2048,512]{1,0:T(8,128)(2,1)}, bf16[2048,512]{1,0:T(8,128)(2,1)}, u32[]{:S(2)}, u32[]{:S(2)}) collective-permute-start(bf16[2048,512]{1,0:T(8,128)(2,1)} %convert_element_type.34), channel_id=1, source_target_pairs={{4,0},{0,4},{5,1},{1,5},{6,2},{2,6},{7,3},{3,7}} | collective-permute-start | bytes 6291464 | tf_op jit(solution)/shard_map/ppermute | solution.py:416
Sparse Core Ops, SparseCore 0:
  60.7 56.6 all-gather.3
  211.7 56.3 all-gather.5
  269.6 55.5 all-gather.7
  628.5 193.7 reduce-scatter.4
  824.8 119.4 reduce-scatter.2

commit v2 on v0

v2 whole, which is shorter than its diff:
```python
import functools

import jax
import jax.numpy as jnp
from jax import lax
from jax.experimental import pallas as pl
from jax.experimental.pallas import tpu as pltpu
from jax.sharding import PartitionSpec as P


F32 = jnp.float32
BF16 = jnp.bfloat16
LIST = 264
GROUP = 8
PER_SRC = 256
TILE = 256
TILE_GROUPS = TILE // GROUP
LANES = 128
STAGE_ROWS = 256
VMEM_LIMIT = 66 * 1000 * 1000


def dot_nn(a, b):
    return lax.dot_general(a, b, (((1,), (0,)), ((), ())), preferred_element_type=F32)


def dot_nt(a, b):
    return lax.dot_general(a, b, (((1,), (1,)), ((), ())), preferred_element_type=F32)


def dot_tn(a, b):
    return lax.dot_general(a, b, (((0,), (0,)), ((), ())), preferred_element_type=F32)


def route_kernel(n_tok, top_k, n_local, n_dev, n_col, base_ref, idx_ref, wts_ref, out_ref, ptr_ref):
    n_list = n_local * LIST
    base = base_ref[0]
    dummy = float(n_tok * n_dev * n_col)

    def first(e):
        return lax.div(e, n_local) * (2 * n_list) + lax.rem(e, n_local) * LIST

    @pl.loop(0, n_local * n_dev)
    def _(e):
        ptr_ref[e] = first(e)

    @pl.loop(0, n_tok // 2)
    def _(i):
        at = i * (2 * top_k)
        experts = [idx_ref[at + j] for j in range(2 * top_k)]
        wts = [wts_ref[at + j] for j in range(2 * top_k)]
        for k in range(2):
            row = ((base + 2 * i + k) * n_col).astype(F32)
            part = slice(k * top_k, (k + 1) * top_k)
            ptrs = [ptr_ref[e] for e in experts[part]]
            for e, p, w in zip(experts[part], ptrs, wts[part]):
                out_ref[p] = row
                out_ref[p + n_list] = w
                ptr_ref[e] = p + 1

    @pl.loop(0, n_local * n_dev)
    def _(e):
        p = ptr_ref[e]
        for k in range(GROUP - 1):
            out_ref[p + k] = dummy
            out_ref[p + k + n_list] = 0.0
        out_ref[first(e) + LIST - 1] = (p - first(e)).astype(F32)


def route_lists(idx, wts, base, n_local, n_dev, n_col):
    n_tok, top_k = idx.shape
    smem = pl.BlockSpec(memory_space=pltpu.SMEM)
    return pl.pallas_call(
        functools.partial(route_kernel, n_tok, top_k, n_local, n_dev, n_col),
        out_shape=jax.ShapeDtypeStruct((n_dev * 2 * n_local * LIST,), F32),
        in_specs=[smem, smem, smem],
        out_specs=smem,
        scratch_shapes=[pltpu.SMEM((n_local * n_dev,), jnp.int32)],
        cost_estimate=pl.CostEstimate(flops=60 * 10**8, bytes_accessed=8 * n_local * n_dev * LIST, transcendentals=0),
        name='route_lists',
    )(base.reshape(1), idx.reshape(n_tok * top_k), wts.reshape(n_tok * top_k))


def load_table(src_hbm, table, stage, sem, n_rows, n_col):
    n_chunk = n_rows // STAGE_ROWS

    def fetch(i):
        slot = lax.rem(i, 2)
        return pltpu.make_async_copy(src_hbm.at[pl.ds(pl.multiple_of(i * STAGE_ROWS, STAGE_ROWS), STAGE_ROWS)], stage.at[slot], sem.at[slot])

    fetch(0).start()

    @pl.loop(0, n_chunk)
    def _(i):
        @pl.when(i + 1 < n_chunk)
        def _():
            fetch(i + 1).start()

        fetch(i).wait()
        rows = stage[lax.rem(i, 2)]
        for c in range(n_col):
            table[pl.ds(i * (STAGE_ROWS * n_col) + c, STAGE_ROWS, stride=n_col), :] = rows[:, c * LANES:(c + 1) * LANES].astype(F32)

    table[pl.ds(n_rows * n_col, 8), :] = jnp.zeros((8, LANES), F32)


SLOT = 4 * (PER_SRC // GROUP) + TILE_GROUPS + 16


def rows_at(first, n_col):
    return pl.ds(pl.multiple_of(first, n_col), n_col)


def n_groups(tok, p, e, n_local):
    return lax.div(tok[(p * n_local + e) * LIST + LIST - 1] + (GROUP - 1), GROUP)


def n_tiles(tok, e, n_src, n_local):
    groups = n_groups(tok, 0, e, n_local)
    for p in range(1, n_src):
        groups = groups + n_groups(tok, p, e, n_local)
    return lax.div(groups + (TILE_GROUPS - 1), TILE_GROUPS)


def list_groups(tok, grp, e, n_src, n_local):
    empty = n_src * n_local * LIST
    at = lax.rem(e, 3) * SLOT
    for p in range(n_src):
        base = (p * n_local + e) * LIST
        groups = n_groups(tok, p, e, n_local)

        @pl.loop(0, lax.div(groups + 3, 4))
        def _(i, base=base, at=at):
            for k in range(4):
                grp[at + 4 * i + k] = base + (4 * i + k) * GROUP

        at = at + groups
    for k in range(TILE_GROUPS):
        grp[at + k] = empty


def start_groups(tok, grp, n_src, n_local):
    for k in range(TILE_GROUPS):
        grp[3 * SLOT + k] = n_src * n_local * LIST
    list_groups(tok, grp, jnp.int32(0), n_src, n_local)


def pick_group(tok, g, tables, bufs, base, row, n_col):
    for k in range(GROUP):
        src = rows_at(tok[base + k], n_col)
        dst = pl.ds(row * n_col + k * n_col, n_col)
        bufs[0][dst, :] = tables[0][src, :]
        if len(tables) > 1:
            bufs[1][dst, :] = tables[1][src, :] * g[base + k]


def add_groups(tok, g, acc, buf, bases, row, n_col):
    dsts, rows = [], []
    for q, base in enumerate(bases):
        for k in range(GROUP):
            dsts.append(rows_at(tok[base + k], n_col))
            val = buf[pl.ds((row + q * GROUP + k) * n_col, n_col), :]
            rows.append(val if g is None else val * g[base + k])
    sums = [acc[d, :] + r for d, r in zip(dsts, rows)]
    for d, r in zip(dsts, sums):
        acc[d, :] = r


def tile_rows(buf, n_col):
    return jnp.concatenate([buf[pl.ds(c, TILE, stride=n_col), :] for c in range(n_col)], axis=1).astype(BF16)


def put_rows(buf, rows, n_col):
    for c in range(n_col):
        buf[pl.ds(c, TILE, stride=n_col), :] = rows[:, c * LANES:(c + 1) * LANES].astype(F32)


def pipelined_tiles(e, n_src, n_local, n_col, tok, g, grp, prev, tables, pick_bufs, acc, out_buf, compute):
    tiles = n_tiles(tok, e, n_src, n_local)
    here = lax.rem(e, 3) * SLOT
    following = lax.rem(e + 1, 3) * SLOT

    @pl.when(e == 0)
    def _():
        prev[0] = 3 * SLOT
        start_groups(tok, grp, n_src, n_local)

        @pl.loop(0, TILE_GROUPS)
        def _(q):
            pick_group(tok, g, tables, pick_bufs, grp[q], pl.multiple_of(q * GROUP, GROUP), n_col)

    list_groups(tok, grp, lax.min(e + 1, n_local - 1), n_src, n_local)

    @pl.loop(0, tiles)
    def _(i):
        last = prev[0]
        coming = jnp.where(i + 1 < tiles, here + (i + 1) * TILE_GROUPS, following)

        def side(part, parts):
            per = TILE_GROUPS // parts
            for q in range(part * per, (part + 1) * per, 2):
                add_groups(tok, g, acc, out_buf, [grp[last + q], grp[last + q + 1]], q * GROUP, n_col)
                for r in (q, q + 1):
                    pick_group(tok, g, tables, pick_bufs, grp[coming + r], r * GROUP, n_col)

        compute(i, side)
        prev[0] = here + i * TILE_GROUPS

    @pl.when(e == n_local - 1)
    def _():
        @pl.loop(0, TILE_GROUPS)
        def _(q):
            add_groups(tok, g, acc, out_buf, [grp[prev[0] + q]], pl.multiple_of(q * GROUP, GROUP), n_col)


def forward_kernel(n_src, n_local, n_rows, n_col, tok, g, x_hbm, dy_hbm, w_one, w_three, w_two, y_hbm, d_ref, x_table, d_table, acc, x_buf, d_buf, out_buf, stage, grp, prev, sem):
    e = pl.program_id(0)

    @pl.when(e == 0)
    def _():
        acc[...] = jnp.zeros_like(acc)
        load_table(x_hbm, x_table, stage, sem, n_rows, n_col)
        load_table(dy_hbm, d_table, stage, sem, n_rows, n_col)

    def compute(i, side):
        rows = pl.ds(pl.multiple_of(i * TILE, TILE), TILE)
        x = tile_rows(x_buf, n_col)
        d_ref[0, rows, :] = tile_rows(d_buf, n_col)
        side(0, 4)
        pre_one = dot_nn(x, w_one[0])
        side(1, 4)
        pre_three = dot_nn(x, w_three[0])
        side(2, 4)
        hidden = (pre_one * jax.nn.sigmoid(pre_one) * pre_three).astype(BF16)
        side(3, 4)
        put_rows(out_buf, dot_nn(hidden, w_two[0]).astype(BF16), n_col)

    pipelined_tiles(e, n_src, n_local, n_col, tok, g, grp, prev, (x_table, d_table), (x_buf, d_buf), acc, out_buf, compute)

    @pl.when(e == n_local - 1)
    def _():
        out = pltpu.make_async_copy(acc.at[pl.ds(0, n_rows * n_col)], y_hbm, sem.at[0])
        out.start()
        out.wait()


def kernel_scratch(n_rows, model, n_table, n_pick):
    n_col = model // LANES
    table = pltpu.VMEM((n_rows * n_col + 8, LANES), F32)
    tile = pltpu.VMEM((TILE * n_col, LANES), F32)
    return [table] * (n_table + 1) + [tile] * (n_pick + 1) + [
        pltpu.VMEM((2, STAGE_ROWS, model), BF16),
        pltpu.SMEM((3 * SLOT + TILE_GROUPS,), jnp.int32),
        pltpu.SMEM((1,), jnp.int32),
        pltpu.SemaphoreType.DMA((2,)),
    ]


def per_expert(a, b):
    return pl.BlockSpec((1, a, b), lambda e: (e, 0, 0))


def forward_partial(tok, g, x_all, dy_all, w_one, w_three, w_two, n_src):
    n_rows, model = x_all.shape
    n_local, _, ffn = w_one.shape
    n_col = model // LANES
    cap = n_src * PER_SRC
    smem = pl.BlockSpec(memory_space=pltpu.SMEM)
    hbm = pl.BlockSpec(memory_space=pl.ANY)
    pairs = n_rows * 8 // n_src
    return pl.pallas_call(
        functools.partial(forward_kernel, n_src, n_local, n_rows, n_col),
        out_shape=(jax.ShapeDtypeStruct((n_rows * n_col, LANES), F32), jax.ShapeDtypeStruct((n_local, cap, model), BF16)),
        grid=(n_local,),
        in_specs=[smem, smem, hbm, hbm, per_expert(model, ffn), per_expert(model, ffn), per_expert(ffn, model)],
        out_specs=(hbm, per_expert(cap, model)),
        scratch_shapes=kernel_scratch(n_rows, model, 2, 2),
        compiler_params=pltpu.CompilerParams(dimension_semantics=('arbitrary',), vmem_limit_bytes=VMEM_LIMIT),
        cost_estimate=pl.CostEstimate(flops=6 * pairs * model * ffn, bytes_accessed=6 * n_local * model * ffn, transcendentals=0),
        name='forward_partial',
    )(tok, g, x_all, dy_all, w_one, w_three, w_two)


def backward_kernel(n_src, n_local, n_rows, n_col, n_part, tok, x_hbm, d_ref, w_one, w_three, w_two, *rest):
    parts, rest = rest[:n_part], rest[n_part:]
    x_ref, h_ref, d1_ref, d3_ref, table, acc, x_buf, out_buf, stage, grp, prev, sem = rest
    e = pl.program_id(0)

    @pl.when(e == 0)
    def _():
        acc[...] = jnp.zeros_like(acc)
        load_table(x_hbm, table, stage, sem, n_rows, n_col)

    def compute(i, side):
        rows = pl.ds(pl.multiple_of(i * TILE, TILE), TILE)
        x = tile_rows(x_buf, n_col)
        x_ref[0, rows, :] = x
        side(0, 4)
        pre_one = dot_nn(x, w_one[0])
        side(1, 4)
        pre_three = dot_nn(x, w_three[0])
        side(2, 4)
        d_hidden = dot_nt(d_ref[0, rows, :], w_two[0]).astype(BF16).astype(F32)
        side(3, 4)
        sig_one = jax.nn.sigmoid(pre_one)
        act_one = pre_one * sig_one
        h_ref[0, rows, :] = (act_one * pre_three).astype(BF16)
        d_three = (d_hidden * act_one).astype(BF16)
        d_one = (d_hidden * pre_three * sig_one * (1.0 + pre_one * (1.0 - sig_one))).astype(BF16)
        d1_ref[0, rows, :] = d_one
        d3_ref[0, rows, :] = d_three
        dx = dot_nt(d_one, w_one[0]) + dot_nt(d_three, w_three[0])
        put_rows(out_buf, dx.astype(BF16), n_col)

    pipelined_tiles(e, n_src, n_local, n_col, tok, None, grp, prev, (table,), (x_buf,), acc, out_buf, compute)

    @pl.when(e == n_local - 1)
    def _():
        own = n_rows * n_col // n_src
        part = own // n_part
        outs = [
            pltpu.make_async_copy(acc.at[pl.ds(q * own + k * part, part)], parts[k].at[pl.ds(q * part, part)], sem.at[0])
            for k in range(n_part) for q in range(n_src)
        ]
        for out in outs:
            out.start()
        for out in outs:
            out.wait()


def backward_partial(tok, x_all, d_rows, w_one, w_three, w_two, n_src, n_part):
    n_rows, model = x_all.shape
    n_local, cap, _ = d_rows.shape
    ffn = w_one.shape[2]
    n_col = model // LANES
    smem = pl.BlockSpec(memory_space=pltpu.SMEM)
    hbm = pl.BlockSpec(memory_space=pl.ANY)
    ffn_out = jax.ShapeDtypeStruct((n_local, cap, ffn), BF16)
    pairs = n_rows * 8 // n_src
    outs = pl.pallas_call(
        functools.partial(backward_kernel, n_src, n_local, n_rows, n_col, n_part),
        out_shape=(jax.ShapeDtypeStruct((n_rows * n_col // n_part, LANES), F32),) * n_part + (jax.ShapeDtypeStruct((n_local, cap, model), BF16), ffn_out, ffn_out, ffn_out),
        grid=(n_local,),
        in_specs=[smem, hbm, per_expert(cap, model), per_expert(model, ffn), per_expert(model, ffn), per_expert(ffn, model)],
        out_specs=(hbm,) * n_part + (per_expert(cap, model), per_expert(cap, ffn), per_expert(cap, ffn), per_expert(cap, ffn)),
        scratch_shapes=kernel_scratch(n_rows, model, 1, 1),
        compiler_params=pltpu.CompilerParams(dimension_semantics=('arbitrary',), vmem_limit_bytes=VMEM_LIMIT),
        cost_estimate=pl.CostEstimate(flops=10 * pairs * model * ffn, bytes_accessed=6 * n_local * cap * ffn, transcendentals=0),
        name='backward_partial',
    )(tok, x_all, d_rows, w_one, w_three, w_two)
    return outs[:n_part], outs[n_part:]


def grad_kernel(n_src, n_local, first, tok, x_ref, d_ref, h_ref, d1_ref, d3_ref, *refs):
    g1_ref, g3_ref, g2_ref = refs[-3:]
    used = n_tiles(tok, pl.program_id(0) + first, n_src, n_local)
    for n in range(1, n_src * PER_SRC // TILE + 1):
        @pl.when(used == n)
        def _(n=n):
            rows = pl.ds(0, n * TILE)
            g1_ref[0] = dot_tn(x_ref[0, rows, :], d1_ref[0, rows, :]).astype(BF16)
            g3_ref[0] = dot_tn(x_ref[0, rows, :], d3_ref[0, rows, :]).astype(BF16)
            g2_ref[0] = dot_tn(h_ref[0, rows, :], d_ref[0, rows, :]).astype(BF16)


def weight_grads(tok, x_rows, d_rows, hidden, d_one, d_three, n_src, first, count, so_far):
    n_local, cap, model = x_rows.shape
    ffn = hidden.shape[2]
    block = lambda a, b: pl.BlockSpec((1, a, b), lambda e: (e + first, 0, 0))
    in_grad = jax.ShapeDtypeStruct((n_local, model, ffn), BF16)
    pairs = count * cap // 2
    return pl.pallas_call(
        functools.partial(grad_kernel, n_src, n_local, first),
        out_shape=(in_grad, in_grad, jax.ShapeDtypeStruct((n_local, ffn, model), BF16)),
        grid=(count,),
        in_specs=[pl.BlockSpec(memory_space=pltpu.SMEM), block(cap, model), block(cap, model), block(cap, ffn), block(cap, ffn), block(cap, ffn)] + [pl.BlockSpec(memory_space=pl.ANY)] * len(so_far),
        out_specs=(block(model, ffn), block(model, ffn), block(ffn, model)),
        input_output_aliases={6 + k: k for k in range(len(so_far))},
        compiler_params=pltpu.CompilerParams(dimension_semantics=('arbitrary',), vmem_limit_bytes=VMEM_LIMIT),
        cost_estimate=pl.CostEstimate(flops=6 * pairs * model * ffn, bytes_accessed=6 * count * cap * ffn, transcendentals=0),
        name='weight_grads',
    )(tok, x_rows, d_rows, hidden, d_one, d_three, *so_far)


def solution(mesh):
    n_stage = mesh.shape['stage']
    n_dev = mesh.shape['expert']
    to_next = [(stage_idx, (stage_idx + 1) % n_stage) for stage_idx in range(n_stage)]
    to_prev = [((stage_idx + 1) % n_stage, stage_idx) for stage_idx in range(n_stage)]
    tok_spec = P('stage', 'expert', None)
    w_spec = P('stage', 'expert', None, None)

    def moe_body(x_act, route_idx, route_wts, w_one, w_three, w_two, dy_act):
        n_tok, model_dim = x_act.shape[1:]
        n_local = w_one.shape[1]
        n_rows = n_tok * n_dev
        n_col = model_dim // LANES
        w_in_one, w_in_three, w_out = w_one[0], w_three[0], w_two[0]

        def gather_tokens(rows):
            return lax.all_gather(rows, 'expert', axis=0, tiled=True)

        def scatter_sums(partial):
            own = lax.psum_scatter(partial, 'expert', scatter_dimension=0, tiled=True)
            return own.reshape(-1, model_dim).astype(BF16)

        x_dst = lax.ppermute(x_act[0], 'stage', to_next)
        idx_dst = lax.ppermute(route_idx[0], 'stage', to_next)
        wts_dst = lax.ppermute(route_wts[0], 'stage', to_next)
        dy_all = gather_tokens(dy_act[0])
        x_dst, idx_dst, wts_dst, x_again = lax.optimization_barrier((x_dst, idx_dst, wts_dst, x_act[0]))
        x_all = gather_tokens(x_dst)
        x_dst_again = lax.ppermute(x_again, 'stage', to_next)
        lists = route_lists(idx_dst, wts_dst, lax.axis_index('expert') * n_tok, n_local, n_dev, n_col)
        n_list = n_local * LIST
        lists = lax.all_to_all(lists.reshape(n_dev, 2 * n_list), 'expert', 0, 0, tiled=True)
        lists, x_dst_again, dy_all, x_all = lax.optimization_barrier((lists, x_dst_again, dy_all, x_all))
        tok = jnp.concatenate([lists[:, :n_list].astype(jnp.int32).reshape(n_dev * n_list), jnp.full((LANES,), n_rows * n_col, jnp.int32)])
        g = jnp.concatenate([lists[:, n_list:].reshape(n_dev * n_list), jnp.zeros((LANES,), F32)])
        x_all_again = gather_tokens(x_dst_again)

        y_sum, d_rows = forward_partial(tok, g, x_all, dy_all, w_in_one, w_in_three, w_out, n_dev)
        y_sum, x_all_again, d_rows = lax.optimization_barrier((y_sum, x_all_again, d_rows))
        y_dst = scatter_sums(y_sum)

        (dx_low, dx_high), (x_rows, hidden, d_one, d_three) = backward_partial(tok, x_all_again, d_rows, w_in_one, w_in_three, w_out, n_dev, 2)
        dx_low = scatter_sums(dx_low)
        dx_high = scatter_sums(dx_high)
        dx_low = lax.ppermute(dx_low, 'stage', to_prev)
        dx_high = lax.ppermute(dx_high, 'stage', to_prev)
        early = n_local * 5 // 8
        grads = weight_grads(tok, x_rows, d_rows, hidden, d_one, d_three, n_dev, 0, early, ())
        g_one, g_three, g_two = weight_grads(tok, x_rows, d_rows, hidden, d_one, d_three, n_dev, early, n_local - early, grads)
        dx_src = jnp.concatenate([dx_low, dx_high])
        return y_dst[None], dx_src[None], g_one[None], g_three[None], g_two[None]

    return jax.shard_map(moe_body, mesh=mesh, in_specs=(tok_spec, tok_spec, tok_spec, w_spec, w_spec, w_spec, tok_spec), out_specs=(tok_spec, tok_spec, w_spec, w_spec, w_spec), check_vma=False)
```

time: 3630 us -> 828 us (0.23)
  local copies, waits for them, and re-layouts: 1300 us -> 12.4 us
  waiting for transfers between devices: 973 us -> 211 us
  matrix products: 756 us -> 0 us
  Pallas kernels: 0 us -> 561 us
  blocking collectives: 379 us -> 9.52 us
  other arithmetic: 149 us -> 8.81 us
  starting transfers between devices: 50.4 us -> 9.58 us
    all_to_all x4 -> x0, waiting for transfers between devices: 922 us -> none  [the longest x2 571 us: combine(): lax.all_to_all(buf_rows, 'expert', 0, 0)]
    gather x6 -> x0, local copies, waits for them, and re-layouts: 845 us -> none  [take_rows(): return jnp.take(row_table, row_ids, axis=0, mode='fill', fill_value=0)]
    dot_general x10 -> x0, matrix products: 756 us -> none  [the longest x1 144 us: expert_backward(): jnp.einsum('pecd,efd->pecf', d_buf, w_out, preferred_element_type=jnp.flo...]
    pallas_call x0 -> x5, Pallas kernels: none -> 561 us  [the longest x1 199 us: backward_partial(): pl.pallas_call(functools.partial(backward_kernel, n_src, n_local, n_rows,...]
    all_to_all x1, blocking collectives: 379 us -> 9.52 us  [moe_body(): lax.all_to_all(lists.reshape(n_dev, 2 * n_list), 'expert', 0, 0, tiled=True)]
    reshape x6 -> x4, local copies, waits for them, and re-layouts: 183 us -> 2.28 us  [the longest x1 1.08 us: route_lists(): idx.reshape(n_tok * top_k)]
    reduce_scatter x0 -> x3, waiting for transfers between devices: none -> 163 us  [scatter_sums(): own = lax.psum_scatter(partial, 'expert', scatter_dimension=0, tiled=True)]
    all_to_all x3 -> x0, local copies, waits for them, and re-layouts: 97.5 us -> none  [the longest x1 51.8 us: dispatch(): return lax.all_to_all(send_buf, 'expert', 0, 0)]
  transfers between devices with their start and end apart: 9 -> 12, of which waited for: 7 -> 5; matrix products, arithmetic and copies ran while one was open for 18% -> 2% of each run, Pallas kernels for 0% -> 44%
where the time goes in v2:
time: 828 us; the launch traced here: 827 us
  Pallas kernels  561 us (68%)
  waiting for transfers between devices  211 us (25%)
  between operations  14.2 us (2%)
  local copies, waits for them, and re-layouts  12.4 us (1%)
  starting transfers between devices  9.58 us (1%)
  blocking collectives  9.52 us (1%)
  other arithmetic  8.81 us (1%)
    pallas_call x1, Pallas kernels, backward_partial(): pl.pallas_call(functools.partial(backward_kernel, n_src, n_local, n_rows,...  199 us
    reduce_scatter x3, waiting for transfers between devices, scatter_sums(): own = lax.psum_scatter(partial, 'expert', scatter_dimension=0, tiled=True)  163 us
    pallas_call x1, Pallas kernels, forward_partial(): pl.pallas_call(functools.partial(forward_kernel, n_src, n_local, n_rows,...  155 us
    pallas_call x2, Pallas kernels, weight_grads(): pl.pallas_call(functools.partial(grad_kernel, n_src, n_local, first), out...  116 us
    pallas_call x1, Pallas kernels, route_lists(): pl.pallas_call(functools.partial(route_kernel, n_tok, top_k, n_local, n_d...  91.8 us
    ppermute x1, waiting for transfers between devices, moe_body(): idx_dst = lax.ppermute(route_idx[0], 'stage', to_next)  45.9 us
  transfers between devices with their start and end apart: 12, of which 5 were waited for; matrix products, arithmetic and copies ran while one was open for 2% of the time, Pallas kernels for 44%

profile of v2, /device:TPU:0, one launch (start us, length us, event | category | flops | bytes accessed | tf_op | source)
XLA Modules:
  0.0 826.6 jit_solution(4762431033587975207)
XLA Ops:
  7.9 3.4 collective-permute-start
  11.3 2.0 collective-permute-start.2
  13.3 45.9 %collective-permute-done.1 = s32[2048,8]{0,1:T(8,128)S(1)} collective-permute-done((s32[2048,8]{0,1:T(8,128)}, s32[2048,8]{0,1:T(8,128)S(1)}, u32[]{:S(2)}, u32[]{:S(2)}) %collective-permute-start.1) | collective-permute-done | bytes 65568 | tf_op jit(solution)/shard_map/ppermute | solution.py:408
  60.0 1.3 copy-done.1
  61.3 1.8 collective-permute-start.3
  63.4 1.1 reshape.46.idx_ref
  65.9 91.8 %route_lists.1 = f32[67584]{0:T(1024)} custom-call(s32[1]{0:T(128)} %bitcast.base_ref, s32[16384]{0:T(1024)} %reshape.46.idx_ref, f32[16384]{0:T(1024)} %reshape.47.wts_ref), custom_call_target="tpu_custom_call" | custom-call | flops 6000000000 | bytes 270336 | tf_op jit(solution)/shard_map/route_lists/pallas_call | solution.py:73
  157.8 9.5 %all_to_all.12 = f32[4,1,16896]{2,1,0:T(1,128)S(1)} all-to-all(f32[4,1,16896]{2,1,0:T(1,128)} %bitcast.21), channel_id=1, replica_groups=mesh['stage'=2,'expert'=4] {'expert'}, dimensions={0} | all-to-all | bytes 540672 | tf_op jit(solution)/shard_map/all_to_all | solution.py:416
  167.5 1.3 copy-done
  170.3 154.6 %forward_partial.1 = (f32[32768,128]{1,0:T(8,128)}, bf16[32,1024,512]{2,1,0:T(8,128)(2,1)}) custom-call(s32[33920]{0:T(1024)} %concatenate.9.tok, f32[33920]{0:T(1024)} %concatenate.10.g, bf16[8192,512]{1,0:T(8,128)(2,1)} %all-gather.5.cloned.1.call-done.x_hbm, bf16[8192,512]{1,0:T(8,128)(2,1)} %bitcast.28, bf16[32,512,768]{2,1,0:T(8,128)(2,1)} %bitcast.22, ...), custom_call_target="tpu_custom_call" | custom-call | flops 38654705664 | bytes 75497472 | tf_op jit(solution)/shard_map/forward_partial/pallas_call | solution.py:271
  324.9 198.9 %backward_partial.1 = (f32[16384,128]{1,0:T(8,128)}, f32[16384,128]{1,0:T(8,128)}, bf16[32,1024,512]{2,1,0:T(8,128)(2,1)}, bf16[32,1024,768]{2,1,0:T(8,128)(2,1)...) custom-call(s32[33920]{0:T(1024)} %concatenate.9.tok, ...), custom_call_target="tpu_custom_call" | custom-call | flops 64424509440 | bytes 150994944 | tf_op jit(solution)/shard_map/backward_partial/pallas_call | solution.py:340
  525.0 68.3 %weight_grads.2 = (bf16[32,512,768]{2,1,0:T(8,128)(2,1)}, bf16[32,512,768]{2,1,0:T(8,128)(2,1)}, bf16[32,768,512]{2,1,0:T(8,128)(2,1)}) custom-call(s32[33920]{0:T(1024)} %concatenate.9.tok, bf16[32,1024,512]{2,1,0:T(8,128)(2,1)} %get-tuple-element.45.x_ref, bf16[32,1024,512]{2,1,0:T(8,128)(2,1)} %get-tuple-element.42.d_ref, ...), custom_call_target="tpu_custom_call" | custom-call | flops 24159191040 | bytes 94371840 | tf_op jit(solution)/shard_map/weight_grads/pallas_call | solution.py:372
  593.3 31.4 %reduce-scatter.6.cloned.1.call-done = f32[4096,128]{1,0:T(8,128)} async-done(((f32[16384,128]{1,0:T(8,128)}), f32[4096,128]{1,0:T(8,128)}) %reduce-scatter.6.cloned.1.call-update) | async-done | bytes 2097168 | tf_op jit(solution)/shard_map/reduce_scatter | solution.py:404
  624.7 1.7 convert_element_type.31
  626.4 1.4 convert_element_type.32
  627.8 65.1 %reduce-scatter.8.cloned.1.call-done = f32[4096,128]{1,0:T(8,128)} async-done(((f32[16384,128]{1,0:T(8,128)}), f32[4096,128]{1,0:T(8,128)}) %reduce-scatter.8.cloned.1.call-update) | async-done | bytes 2097168 | tf_op jit(solution)/shard_map/reduce_scatter | solution.py:404
  692.9 1.7 convert_element_type.33
  694.6 1.4 convert_element_type.34
  696.1 1.5 collective-permute-start.5
  698.1 47.3 %weight_grads.3 = (bf16[32,512,768]{2,1,0:T(8,128)(2,1)}, bf16[32,512,768]{2,1,0:T(8,128)(2,1)}, bf16[32,768,512]{2,1,0:T(8,128)(2,1)}) custom-call(s32[33920]{0:T(1024)} %concatenate.9.tok, bf16[32,1024,512]{2,1,0:T(8,128)(2,1)} %get-tuple-element.45.x_ref, ...), custom_call_target="tpu_custom_call", output_to_operand_aliasing={{0}: (6, {}), {1}: (7, {}), {2}: (8, {})} | custom-call | flops 14495514624 | bytes 56623104 | tf_op jit(solution)/shard_map/weight_grads/pallas_call | solution.py:372
  745.4 3.0 maximum_bitcast_fusion
  748.4 66.5 %reduce-scatter.4.cloned.1.call-done = f32[8192,128]{1,0:T(8,128)} async-done(((f32[32768,128]{1,0:T(8,128)}), f32[8192,128]{1,0:T(8,128)}) %reduce-scatter.4.cloned.1.call-update) | async-done | bytes 4194320 | tf_op jit(solution)/shard_map/reduce_scatter | solution.py:404
  814.9 2.4 convert_element_type.29
  817.2 2.6 convert_element_type.30
  (33 shorter events, 6.6 us)
Async XLA Ops:
  7.2 160.3 %all-gather.9.cloned.1.call-start = ((), (), s32[]{:S(2)}) async-start(), calls=%async_computation.9 | async-start | bytes 10485760 | tf_op jit(solution)/shard_map/all_gather | solution.py:401
  7.9 159.6 %all-gather.5.cloned.1.call-start = ((), (), s32[]{:S(2)}) async-start(), calls=%async_computation.4 | async-start | bytes 10485760 | tf_op jit(solution)/shard_map/all_gather | solution.py:401
  7.9 52.0 %collective-permute-start = (bf16[2048,512]{1,0:T(8,128)(2,1)}, bf16[2048,512]{1,0:T(8,128)(2,1)S(1)}, u32[]{:S(2)}, u32[]{:S(2)}) collective-permute-start(bf16[2048,512]{1,0:T(8,128)(2,1)} %bitcast.29), channel_id=1, source_target_pairs={{0,4},{4,0},{1,5},{5,1},{2,6},{6,2},{3,7},{7,3}} | collective-permute-start | bytes 6291464 | tf_op jit(solution)/shard_map/ppermute | solution.py:407
  11.3 47.9 %collective-permute-start.1 = (s32[2048,8]{0,1:T(8,128)}, s32[2048,8]{0,1:T(8,128)S(1)}, u32[]{:S(2)}, u32[]{:S(2)}) collective-permute-start(s32[2048,8]{0,1:T(8,128)} %bitcast.31), channel_id=1, source_target_pairs={{0,4},{4,0},{1,5},{5,1},{2,6},{6,2},{3,7},{7,3}} | collective-permute-start | bytes 196616 | tf_op jit(solution)/shard_map/ppermute | solution.py:408
  11.3 48.6 %collective-permute-start.2 = (f32[2048,8]{0,1:T(8,128)}, f32[2048,8]{0,1:T(8,128)S(1)}, u32[]{:S(2)}, u32[]{:S(2)}) collective-permute-start(f32[2048,8]{0,1:T(8,128)} %bitcast.32), channel_id=1, source_target_pairs={{0,4},{4,0},{1,5},{5,1},{2,6},{6,2},{3,7},{7,3}} | collective-permute-start | bytes 196616 | tf_op jit(solution)/shard_map/ppermute | solution.py:409
  60.0 1.3 copy-start.1
  61.3 263.6 %all-gather.7.cloned.1.call-start = ((), (), s32[]{:S(2)}) async-start(), calls=%async_computation.5 | async-start | bytes 10485760 | tf_op jit(solution)/shard_map/all_gather | solution.py:401
  61.3 106.0 %collective-permute-start.3 = (bf16[2048,512]{1,0:T(8,128)(2,1)}, bf16[2048,512]{1,0:T(8,128)(2,1)S(1)}, u32[]{:S(2)}, u32[]{:S(2)}) collective-permute-start(bf16[2048,512]{1,0:T(8,128)(2,1)} %bitcast.30), channel_id=1, source_target_pairs={{0,4},{4,0},{1,5},{5,1},{2,6},{6,2},{3,7},{7,3}} | collective-permute-start | bytes 6291464 | tf_op jit(solution)/shard_map/ppermute | solution.py:413
  167.4 1.3 copy-start
  168.7 455.9 %reduce-scatter.6.cloned.1.call-start = ((), (), s32[]{:S(2)}) async-start(), calls=%async_computation.7 | async-start | bytes 10485760 | tf_op jit(solution)/shard_map/reduce_scatter | solution.py:404
  523.9 169.1 %reduce-scatter.8.cloned.1.call-start = ((), (), s32[]{:S(2)}) async-start(), calls=%async_computation.8 | async-start | bytes 10485760 | tf_op jit(solution)/shard_map/reduce_scatter | solution.py:404
  524.4 290.4 %reduce-scatter.4.cloned.1.call-start = ((), (), s32[]{:S(2)}) async-start(), calls=%async_computation.6 | async-start | bytes 20971520 | tf_op jit(solution)/shard_map/reduce_scatter | solution.py:404
  696.1 49.3 %collective-permute-start.5 = (bf16[1024,512]{1,0:T(8,128)(2,1)}, bf16[1024,512]{1,0:T(8,128)(2,1)}, u32[]{:S(2)}, u32[]{:S(2)}) collective-permute-start(bf16[1024,512]{1,0:T(8,128)(2,1)} %convert_element_type.34), channel_id=1, source_target_pairs={{4,0},{0,4},{5,1},{1,5},{6,2},{2,6},{7,3},{3,7}} | collective-permute-start | bytes 3145736 | tf_op jit(solution)/shard_map/ppermute | solution.py:430
  697.6 47.8 %collective-permute-start.4 = (bf16[1024,512]{1,0:T(8,128)(2,1)}, bf16[1024,512]{1,0:T(8,128)(2,1)}, u32[]{:S(2)}, u32[]{:S(2)}) collective-permute-start(bf16[1024,512]{1,0:T(8,128)(2,1)} %convert_element_type.32), channel_id=1, source_target_pairs={{4,0},{0,4},{5,1},{1,5},{6,2},{2,6},{7,3},{3,7}} | collective-permute-start | bytes 3145736 | tf_op jit(solution)/shard_map/ppermute | solution.py:429
Sparse Core Ops, SparseCore 0:
  9.5 58.2 all-gather.8
  69.9 55.4 all-gather.4
  168.9 54.3 all-gather.6
  524.0 100.6 reduce-scatter.5
  627.1 65.8 reduce-scatter.7
  695.3 119.4 reduce-scatter.3

commit v3 on v2

--- a/solution.py
+++ b/solution.py
@@ -16,7 +16,9 @@
 TILE = 256
 TILE_GROUPS = TILE // GROUP
 LANES = 128
-STAGE_ROWS = 256
+SUB = 4
+STAGE_ROWS = 128
+STAGE_SLOTS = 8
 VMEM_LIMIT = 66 * 1000 * 1000
 
 
@@ -32,30 +34,24 @@
     return lax.dot_general(a, b, (((0,), (0,)), ((), ())), preferred_element_type=F32)
 
 
-def route_kernel(n_tok, top_k, n_local, n_dev, n_col, base_ref, idx_ref, wts_ref, out_ref, ptr_ref):
-    n_list = n_local * LIST
-    base = base_ref[0]
-    dummy = float(n_tok * n_dev * n_col)
-
-    def first(e):
-        return lax.div(e, n_local) * (2 * n_list) + lax.rem(e, n_local) * LIST
+def route_kernel(n_tok, top_k, n_local, n_dev, dummy, idx_ref, val_ref, out_ref, ptr_ref):
+    per_pair = val_ref.shape[0] > 1
 
     @pl.loop(0, n_local * n_dev)
     def _(e):
-        ptr_ref[e] = first(e)
-
-    @pl.loop(0, n_tok // 2)
-    def _(i):
-        at = i * (2 * top_k)
-        experts = [idx_ref[at + j] for j in range(2 * top_k)]
-        wts = [wts_ref[at + j] for j in range(2 * top_k)]
-        for k in range(2):
-            row = ((base + 2 * i + k) * n_col).astype(F32)
-            part = slice(k * top_k, (k + 1) * top_k)
-            ptrs = [ptr_ref[e] for e in experts[part]]
-            for e, p, w in zip(experts[part], ptrs, wts[part]):
-                out_ref[p] = row
-                out_ref[p + n_list] = w
+        ptr_ref[e] = e * LIST
+
+    @pl.loop(0, n_tok)
+    def _(t):
+        token = None if per_pair else (val_ref[0] + t) * SUB
+        half = top_k // 2
+        for part in range(2):
+            at = t * top_k + part * half
+            experts = [idx_ref[at + j] for j in range(half)]
+            ptrs = [ptr_ref[e] for e in experts]
+            vals = [val_ref[at + j] if per_pair else token for j in range(half)]
+            for e, p, v in zip(experts, ptrs, vals):
+                out_ref[p] = v
                 ptr_ref[e] = p + 1
 
     @pl.loop(0, n_local * n_dev)
@@ -63,43 +59,43 @@
         p = ptr_ref[e]
         for k in range(GROUP - 1):
             out_ref[p + k] = dummy
-            out_ref[p + k + n_list] = 0.0
-        out_ref[first(e) + LIST - 1] = (p - first(e)).astype(F32)
-
-
-def route_lists(idx, wts, base, n_local, n_dev, n_col):
-    n_tok, top_k = idx.shape
+        out_ref[e * LIST + LIST - 1] = (p - e * LIST).astype(out_ref.dtype)
+
+
+def route_lists(idx, vals, n_tok, n_local, n_dev, dummy):
+    n_pair = idx.shape[0]
     smem = pl.BlockSpec(memory_space=pltpu.SMEM)
     return pl.pallas_call(
-        functools.partial(route_kernel, n_tok, top_k, n_local, n_dev, n_col),
-        out_shape=jax.ShapeDtypeStruct((n_dev * 2 * n_local * LIST,), F32),
-        in_specs=[smem, smem, smem],
+        functools.partial(route_kernel, n_tok, n_pair // n_tok, n_local, n_dev, dummy),
+        out_shape=jax.ShapeDtypeStruct((n_dev * n_local * LIST,), vals.dtype),
+        in_specs=[smem, smem],
         out_specs=smem,
         scratch_shapes=[pltpu.SMEM((n_local * n_dev,), jnp.int32)],
-        cost_estimate=pl.CostEstimate(flops=60 * 10**8, bytes_accessed=8 * n_local * n_dev * LIST, transcendentals=0),
+        cost_estimate=pl.CostEstimate(flops=40 * 10**8, bytes_accessed=8 * n_local * n_dev * LIST, transcendentals=0),
         name='route_lists',
-    )(base.reshape(1), idx.reshape(n_tok * top_k), wts.reshape(n_tok * top_k))
+    )(idx, vals)
 
 
 def load_table(src_hbm, table, stage, sem, n_rows, n_col):
     n_chunk = n_rows // STAGE_ROWS
 
     def fetch(i):
-        slot = lax.rem(i, 2)
+        slot = lax.rem(i, STAGE_SLOTS)
         return pltpu.make_async_copy(src_hbm.at[pl.ds(pl.multiple_of(i * STAGE_ROWS, STAGE_ROWS), STAGE_ROWS)], stage.at[slot], sem.at[slot])
 
-    fetch(0).start()
+    for k in range(min(STAGE_SLOTS, n_chunk)):
+        fetch(jnp.int32(k)).start()
 
     @pl.loop(0, n_chunk)
     def _(i):
-        @pl.when(i + 1 < n_chunk)
-        def _():
-            fetch(i + 1).start()
-
         fetch(i).wait()
-        rows = stage[lax.rem(i, 2)]
+        rows = stage[lax.rem(i, STAGE_SLOTS)]
         for c in range(n_col):
             table[pl.ds(i * (STAGE_ROWS * n_col) + c, STAGE_ROWS, stride=n_col), :] = rows[:, c * LANES:(c + 1) * LANES].astype(F32)
+
+        @pl.when(i + STAGE_SLOTS < n_chunk)
+        def _():
+            fetch(i + STAGE_SLOTS).start()
 
     table[pl.ds(n_rows * n_col, 8), :] = jnp.zeros((8, LANES), F32)
 
@@ -213,14 +209,21 @@
             add_groups(tok, g, acc, out_buf, [grp[prev[0] + q]], pl.multiple_of(q * GROUP, GROUP), n_col)
 
 
-def forward_kernel(n_src, n_local, n_rows, n_col, tok, g, x_hbm, dy_hbm, w_one, w_three, w_two, y_hbm, d_ref, x_table, d_table, acc, x_buf, d_buf, out_buf, stage, grp, prev, sem):
+def forward_kernel(n_src, n_local, n_rows, n_col, tok_hbm, g_hbm, x_hbm, dy_hbm, w_one, w_three, w_two, y_hbm, d_ref, tiles_ref, x_table, d_table, acc, x_buf, d_buf, out_buf, stage, grp, prev, sem, list_sem, tok, g):
     e = pl.program_id(0)
 
     @pl.when(e == 0)
     def _():
+        lists = [pltpu.make_async_copy(tok_hbm, tok, list_sem.at[0]), pltpu.make_async_copy(g_hbm, g, list_sem.at[1])]
+        for copy in lists:
+            copy.start()
         acc[...] = jnp.zeros_like(acc)
         load_table(x_hbm, x_table, stage, sem, n_rows, n_col)
         load_table(dy_hbm, d_table, stage, sem, n_rows, n_col)
+        for copy in lists:
+            copy.wait()
+
+    tiles_ref[e] = n_tiles(tok, e, n_src, n_local)
 
     def compute(i, side):
         rows = pl.ds(pl.multiple_of(i * TILE, TILE), TILE)
@@ -249,9 +252,10 @@
     table = pltpu.VMEM((n_rows * n_col + 8, LANES), F32)
     tile = pltpu.VMEM((TILE * n_col, LANES), F32)
     return [table] * (n_table + 1) + [tile] * (n_pick + 1) + [
-        pltpu.VMEM((2, STAGE_ROWS, model), BF16),
+        pltpu.VMEM((STAGE_SLOTS, STAGE_ROWS, model), BF16),
         pltpu.SMEM((3 * SLOT + TILE_GROUPS,), jnp.int32),
         pltpu.SMEM((1,), jnp.int32),
+        pltpu.SemaphoreType.DMA((STAGE_SLOTS,)),
         pltpu.SemaphoreType.DMA((2,)),
     ]
 
@@ -270,26 +274,29 @@
     pairs = n_rows * 8 // n_src
     return pl.pallas_call(
         functools.partial(forward_kernel, n_src, n_local, n_rows, n_col),
-        out_shape=(jax.ShapeDtypeStruct((n_rows * n_col, LANES), F32), jax.ShapeDtypeStruct((n_local, cap, model), BF16)),
+        out_shape=(jax.ShapeDtypeStruct((n_rows * n_col, LANES), F32), jax.ShapeDtypeStruct((n_local, cap, model), BF16), jax.ShapeDtypeStruct((n_local,), jnp.int32)),
         grid=(n_local,),
-        in_specs=[smem, smem, hbm, hbm, per_expert(model, ffn), per_expert(model, ffn), per_expert(ffn, model)],
-        out_specs=(hbm, per_expert(cap, model)),
-        scratch_shapes=kernel_scratch(n_rows, model, 2, 2),
+        in_specs=[hbm, hbm, hbm, hbm, per_expert(model, ffn), per_expert(model, ffn), per_expert(ffn, model)],
+        out_specs=(hbm, per_expert(cap, model), smem),
+        scratch_shapes=kernel_scratch(n_rows, model, 2, 2) + [pltpu.SMEM(tok.shape, tok.dtype), pltpu.SMEM(g.shape, g.dtype)],
         compiler_params=pltpu.CompilerParams(dimension_semantics=('arbitrary',), vmem_limit_bytes=VMEM_LIMIT),
         cost_estimate=pl.CostEstimate(flops=6 * pairs * model * ffn, bytes_accessed=6 * n_local * model * ffn, transcendentals=0),
         name='forward_partial',
     )(tok, g, x_all, dy_all, w_one, w_three, w_two)
 
 
-def backward_kernel(n_src, n_local, n_rows, n_col, n_part, tok, x_hbm, d_ref, w_one, w_three, w_two, *rest):
+def backward_kernel(n_src, n_local, n_rows, n_col, n_part, tok_hbm, x_hbm, d_ref, w_one, w_three, w_two, *rest):
     parts, rest = rest[:n_part], rest[n_part:]
-    x_ref, h_ref, d1_ref, d3_ref, table, acc, x_buf, out_buf, stage, grp, prev, sem = rest
+    x_ref, h_ref, d1_ref, d3_ref, table, acc, x_buf, out_buf, stage, grp, prev, sem, list_sem, tok = rest
     e = pl.program_id(0)
 
     @pl.when(e == 0)
     def _():
+        lists = pltpu.make_async_copy(tok_hbm, tok, list_sem.at[0])
+        lists.start()
         acc[...] = jnp.zeros_like(acc)
         load_table(x_hbm, table, stage, sem, n_rows, n_col)
+        lists.wait()
 
     def compute(i, side):
         rows = pl.ds(pl.multiple_of(i * TILE, TILE), TILE)
@@ -333,7 +340,6 @@
     n_local, cap, _ = d_rows.shape
     ffn = w_one.shape[2]
     n_col = model // LANES
-    smem = pl.BlockSpec(memory_space=pltpu.SMEM)
     hbm = pl.BlockSpec(memory_space=pl.ANY)
     ffn_out = jax.ShapeDtypeStruct((n_local, cap, ffn), BF16)
     pairs = n_rows * 8 // n_src
@@ -341,9 +347,9 @@
         functools.partial(backward_kernel, n_src, n_local, n_rows, n_col, n_part),
         out_shape=(jax.ShapeDtypeStruct((n_rows * n_col // n_part, LANES), F32),) * n_part + (jax.ShapeDtypeStruct((n_local, cap, model), BF16), ffn_out, ffn_out, ffn_out),
         grid=(n_local,),
-        in_specs=[smem, hbm, per_expert(cap, model), per_expert(model, ffn), per_expert(model, ffn), per_expert(ffn, model)],
+        in_specs=[hbm, hbm, per_expert(cap, model), per_expert(model, ffn), per_expert(model, ffn), per_expert(ffn, model)],
         out_specs=(hbm,) * n_part + (per_expert(cap, model), per_expert(cap, ffn), per_expert(cap, ffn), per_expert(cap, ffn)),
-        scratch_shapes=kernel_scratch(n_rows, model, 1, 1),
+        scratch_shapes=kernel_scratch(n_rows, model, 1, 1) + [pltpu.SMEM(tok.shape, tok.dtype)],
         compiler_params=pltpu.CompilerParams(dimension_semantics=('arbitrary',), vmem_limit_bytes=VMEM_LIMIT),
         cost_estimate=pl.CostEstimate(flops=10 * pairs * model * ffn, bytes_accessed=6 * n_local * cap * ffn, transcendentals=0),
         name='backward_partial',
@@ -351,9 +357,9 @@
     return outs[:n_part], outs[n_part:]
 
 
-def grad_kernel(n_src, n_local, first, tok, x_ref, d_ref, h_ref, d1_ref, d3_ref, *refs):
+def grad_kernel(n_src, first, tiles, x_ref, d_ref, h_ref, d1_ref, d3_ref, *refs):
     g1_ref, g3_ref, g2_ref = refs[-3:]
-    used = n_tiles(tok, pl.program_id(0) + first, n_src, n_local)
+    used = tiles[pl.program_id(0) + first]
     for n in range(1, n_src * PER_SRC // TILE + 1):
         @pl.when(used == n)
         def _(n=n):
@@ -363,14 +369,14 @@
             g2_ref[0] = dot_tn(h_ref[0, rows, :], d_ref[0, rows, :]).astype(BF16)
 
 
-def weight_grads(tok, x_rows, d_rows, hidden, d_one, d_three, n_src, first, count, so_far):
+def weight_grads(tiles, x_rows, d_rows, hidden, d_one, d_three, n_src, first, count, so_far):
     n_local, cap, model = x_rows.shape
     ffn = hidden.shape[2]
     block = lambda a, b: pl.BlockSpec((1, a, b), lambda e: (e + first, 0, 0))
     in_grad = jax.ShapeDtypeStruct((n_local, model, ffn), BF16)
     pairs = count * cap // 2
     return pl.pallas_call(
-        functools.partial(grad_kernel, n_src, n_local, first),
+        functools.partial(grad_kernel, n_src, first),
         out_shape=(in_grad, in_grad, jax.ShapeDtypeStruct((n_local, ffn, model), BF16)),
         grid=(count,),
         in_specs=[pl.BlockSpec(memory_space=pltpu.SMEM), block(cap, model), block(cap, model), block(cap, ffn), block(cap, ffn), block(cap, ffn)] + [pl.BlockSpec(memory_space=pl.ANY)] * len(so_far),
@@ -379,7 +385,7 @@
         compiler_params=pltpu.CompilerParams(dimension_semantics=('arbitrary',), vmem_limit_bytes=VMEM_LIMIT),
         cost_estimate=pl.CostEstimate(flops=6 * pairs * model * ffn, bytes_accessed=6 * count * cap * ffn, transcendentals=0),
         name='weight_grads',
-    )(tok, x_rows, d_rows, hidden, d_one, d_three, *so_far)
+    )(tiles, x_rows, d_rows, hidden, d_one, d_three, *so_far)
 
 
 def solution(mesh):
@@ -404,22 +410,29 @@
             own = lax.psum_scatter(partial, 'expert', scatter_dimension=0, tiled=True)
             return own.reshape(-1, model_dim).astype(BF16)
 
-        x_dst = lax.ppermute(x_act[0], 'stage', to_next)
+        n_list = n_local * LIST
+
+        def to_experts(lists, dummy):
+            lists = lax.all_to_all(lists.reshape(n_dev, n_list), 'expert', 0, 0, tiled=True)
+            return jnp.concatenate([lists.reshape(n_dev * n_list), jnp.full((LANES,), dummy, lists.dtype)])
+
         idx_dst = lax.ppermute(route_idx[0], 'stage', to_next)
         wts_dst = lax.ppermute(route_wts[0], 'stage', to_next)
+        x_dst = lax.ppermute(x_act[0], 'stage', to_next)
         dy_all = gather_tokens(dy_act[0])
-        x_dst, idx_dst, wts_dst, x_again = lax.optimization_barrier((x_dst, idx_dst, wts_dst, x_act[0]))
+        idx_dst = idx_dst.reshape(-1)
+        wts_dst = wts_dst.reshape(-1)
+        first_row = (lax.axis_index('expert') * n_tok).reshape(1)
+        tok = route_lists(idx_dst, first_row, n_tok, n_local, n_dev, n_rows * n_col)
+        x_dst, tok, idx_dst, wts_dst, x_again = lax.optimization_barrier((x_dst, tok, idx_dst, wts_dst, x_act[0]))
         x_all = gather_tokens(x_dst)
         x_dst_again = lax.ppermute(x_again, 'stage', to_next)
-        lists = route_lists(idx_dst, wts_dst, lax.axis_index('expert') * n_tok, n_local, n_dev, n_col)
-        n_list = n_local * LIST
-        lists = lax.all_to_all(lists.reshape(n_dev, 2 * n_list), 'expert', 0, 0, tiled=True)
-        lists, x_dst_again, dy_all, x_all = lax.optimization_barrier((lists, x_dst_again, dy_all, x_all))
-        tok = jnp.concatenate([lists[:, :n_list].astype(jnp.int32).reshape(n_dev * n_list), jnp.full((LANES,), n_rows * n_col, jnp.int32)])
-        g = jnp.concatenate([lists[:, n_list:].reshape(n_dev * n_list), jnp.zeros((LANES,), F32)])
+        g = route_lists(idx_dst, wts_dst, n_tok, n_local, n_dev, 0.0)
+        tok, g = to_experts(tok, n_rows * n_col), to_experts(g, 0.0)
+        tok, g, x_dst_again, dy_all, x_all = lax.optimization_barrier((tok, g, x_dst_again, dy_all, x_all))
         x_all_again = gather_tokens(x_dst_again)
 
-        y_sum, d_rows = forward_partial(tok, g, x_all, dy_all, w_in_one, w_in_three, w_out, n_dev)
+        y_sum, d_rows, tiles = forward_partial(tok, g, x_all, dy_all, w_in_one, w_in_three, w_out, n_dev)
         y_sum, x_all_again, d_rows = lax.optimization_barrier((y_sum, x_all_again, d_rows))
         y_dst = scatter_sums(y_sum)
 
@@ -429,8 +442,8 @@
         dx_low = lax.ppermute(dx_low, 'stage', to_prev)
         dx_high = lax.ppermute(dx_high, 'stage', to_prev)
         early = n_local * 5 // 8
-        grads = weight_grads(tok, x_rows, d_rows, hidden, d_one, d_three, n_dev, 0, early, ())
-        g_one, g_three, g_two = weight_grads(tok, x_rows, d_rows, hidden, d_one, d_three, n_dev, early, n_local - early, grads)
+        grads = weight_grads(tiles, x_rows, d_rows, hidden, d_one, d_three, n_dev, 0, early, ())
+        g_one, g_three, g_two = weight_grads(tiles, x_rows, d_rows, hidden, d_one, d_three, n_dev, early, n_local - early, grads)
         dx_src = jnp.concatenate([dx_low, dx_high])
         return y_dst[None], dx_src[None], g_one[None], g_three[None], g_two[None]
 

time: 828 us -> 808 us (0.976)
  Pallas kernels: 561 us -> 540 us
  blocking collectives: 9.52 us -> 0 us
    ppermute x1, waiting for transfers between devices: 45.9 us -> 0.01 us  [moe_body(): idx_dst = lax.ppermute(route_idx[0], 'stage', to_next)]
    ppermute x1, waiting for transfers between devices: 0.7 us -> 45.9 us  [moe_body(): wts_dst = lax.ppermute(route_wts[0], 'stage', to_next)]
    pallas_call x1, Pallas kernels: 155 us -> 131 us  [forward_partial(): pl.pallas_call(functools.partial(forward_kernel, n_src, n_local, n_rows,...]
    pallas_call x3 -> x4, Pallas kernels: 207 us -> 222 us  [the longest x2 115 us: weight_grads(): pl.pallas_call(functools.partial(grad_kernel, n_src, first), out_shape=(i...]
    pallas_call x1, Pallas kernels: 199 us -> 187 us  [backward_partial(): pl.pallas_call(functools.partial(backward_kernel, n_src, n_local, n_rows,...]
    all_to_all x1 -> x0, blocking collectives: 9.52 us -> none  [moe_body(): lax.all_to_all(lists.reshape(n_dev, 2 * n_list), 'expert', 0, 0, tiled=True)]
  transfers between devices with their start and end apart: 12 -> 14, of which waited for: 5 -> 5; matrix products, arithmetic and copies ran while one was open for 2% -> 2% of each run, Pallas kernels for 44% -> 44%
where the time goes in v3:
time: 808 us; the launch traced here: 806 us
  Pallas kernels  540 us (67%)
  waiting for transfers between devices  215 us (27%)
  starting transfers between devices  16.1 us (2%)
  between operations  14.2 us (2%)
  local copies, waits for them, and re-layouts  12.2 us (2%)
  other arithmetic  8.77 us (1%)
    pallas_call x1, Pallas kernels, backward_partial(): pl.pallas_call(functools.partial(backward_kernel, n_src, n_local, n_rows,...  187 us
    reduce_scatter x3, waiting for transfers between devices, scatter_sums(): own = lax.psum_scatter(partial, 'expert', scatter_dimension=0, tiled=True)  163 us
    pallas_call x1, Pallas kernels, forward_partial(): pl.pallas_call(functools.partial(forward_kernel, n_src, n_local, n_rows,...  131 us
    pallas_call x2, Pallas kernels, weight_grads(): pl.pallas_call(functools.partial(grad_kernel, n_src, first), out_shape=(i...  115 us
    pallas_call x2, Pallas kernels, route_lists(): pl.pallas_call(functools.partial(route_kernel, n_tok, n_pair // n_tok, n_...  107 us
    ppermute x1, waiting for transfers between devices, moe_body(): wts_dst = lax.ppermute(route_wts[0], 'stage', to_next)  45.9 us
  transfers between devices with their start and end apart: 14, of which 5 were waited for; matrix products, arithmetic and copies ran while one was open for 2% of the time, Pallas kernels for 44%

profile of v3, /device:TPU:0, one launch (start us, length us, event | category | flops | bytes accessed | tf_op | source)
XLA Modules:
  0.0 806.2 jit_solution(3254380128236398467)
XLA Ops:
  7.9 3.4 collective-permute-start
  11.3 2.0 collective-permute-start.1
  13.3 45.9 %collective-permute-done.2 = f32[2048,8]{0,1:T(8,128)S(1)} collective-permute-done((f32[2048,8]{0,1:T(8,128)}, f32[2048,8]{0,1:T(8,128)S(1)}, u32[]{:S(2)}, u32[]{:S(2)}) %collective-permute-start.2) | collective-permute-done | bytes 65568 | tf_op jit(solution)/shard_map/ppermute | solution.py:420
  62.1 53.0 %route_lists.2 = s32[33792]{0:T(1024)} custom-call(s32[16384]{0:T(1024)} %reshape.51.idx_ref, s32[1]{0:T(128)} %bitcast.2.val_ref), custom_call_target="tpu_custom_call" | custom-call | flops 4000000000 | bytes 270336 | tf_op jit(solution)/shard_map/route_lists/pallas_call | solution.py:68
  116.4 1.8 collective-permute-start.3
  118.2 3.3 all-to-all-start
  121.5 54.1 %route_lists.3 = f32[33792]{0:T(1024)} custom-call(s32[16384]{0:T(1024)} %reshape.51.idx_ref, f32[16384]{0:T(1024)} %reshape.53.val_ref), custom_call_target="tpu_custom_call" | custom-call | flops 4000000000 | bytes 270336 | tf_op jit(solution)/shard_map/route_lists/pallas_call | solution.py:68
  175.6 3.3 all-to-all-start.1
  179.7 3.9 all-to-all-done.1
  185.7 131.2 %forward_partial.1 = (f32[32768,128]{1,0:T(8,128)}, bf16[32,1024,512]{2,1,0:T(8,128)(2,1)}, s32[32]{0:T(128)}) custom-call(s32[33920]{0:T(1024)} %concatenate.9.tok_hbm, f32[33920]{0:T(1024)} %concatenate.10.g_hbm, bf16[8192,512]{1,0:T(8,128)(2,1)} %all-gather.5.cloned.1.call-done.x_hbm, bf16[8192,512]{1,0:T(8,128)(2,1)} %bitcast.30, ...), custom_call_target="tpu_custom_call" | custom-call | flops 38654705664 | bytes 75497472 | tf_op jit(solution)/shard_map/forward_partial/pallas_call | solution.py:275
  317.0 186.7 %backward_partial.1 = (f32[16384,128]{1,0:T(8,128)}, f32[16384,128]{1,0:T(8,128)}, bf16[32,1024,512]{2,1,0:T(8,128)(2,1)}, bf16[32,1024,768]{2,1,0:T(8,128)(2,1)...) custom-call(s32[33920]{0:T(1024)} %concatenate.9.tok_hbm, ...), custom_call_target="tpu_custom_call" | custom-call | flops 64424509440 | bytes 150994944 | tf_op jit(solution)/shard_map/backward_partial/pallas_call | solution.py:346
  504.8 67.9 %weight_grads.2 = (bf16[32,512,768]{2,1,0:T(8,128)(2,1)}, bf16[32,512,768]{2,1,0:T(8,128)(2,1)}, bf16[32,768,512]{2,1,0:T(8,128)(2,1)}) custom-call(s32[32]{0:T(128)} %get-tuple-element.50.tiles, bf16[32,1024,512]{2,1,0:T(8,128)(2,1)} %get-tuple-element.51.x_ref, bf16[32,1024,512]{2,1,0:T(8,128)(2,1)} %get-tuple-element.47.d_ref, ...), custom_call_target="tpu_custom_call" | custom-call | flops 24159191040 | bytes 94371840 | tf_op jit(solution)/shard_map/weight_grads/pallas_call | solution.py:378
  572.8 31.4 %reduce-scatter.6.cloned.1.call-done = f32[4096,128]{1,0:T(8,128)} async-done(((f32[16384,128]{1,0:T(8,128)}), f32[4096,128]{1,0:T(8,128)}) %reduce-scatter.6.cloned.1.call-update) | async-done | bytes 2097168 | tf_op jit(solution)/shard_map/reduce_scatter | solution.py:410
  604.2 1.7 convert_element_type.27
  605.9 1.4 convert_element_type.28
  607.4 65.1 %reduce-scatter.8.cloned.1.call-done = f32[4096,128]{1,0:T(8,128)} async-done(((f32[16384,128]{1,0:T(8,128)}), f32[4096,128]{1,0:T(8,128)}) %reduce-scatter.8.cloned.1.call-update) | async-done | bytes 2097168 | tf_op jit(solution)/shard_map/reduce_scatter | solution.py:410
  672.5 1.7 convert_element_type.29
  674.2 1.4 convert_element_type.30
  675.6 1.5 collective-permute-start.5
  677.7 47.2 %weight_grads.3 = (bf16[32,512,768]{2,1,0:T(8,128)(2,1)}, bf16[32,512,768]{2,1,0:T(8,128)(2,1)}, bf16[32,768,512]{2,1,0:T(8,128)(2,1)}) custom-call(s32[32]{0:T(128)} %get-tuple-element.50.tiles, bf16[32,1024,512]{2,1,0:T(8,128)(2,1)} %get-tuple-element.51.x_ref, ...), custom_call_target="tpu_custom_call", output_to_operand_aliasing={{0}: (6, {}), {1}: (7, {}), {2}: (8, {})} | custom-call | flops 14495514624 | bytes 56623104 | tf_op jit(solution)/shard_map/weight_grads/pallas_call | solution.py:378
  724.9 3.0 maximum_bitcast_fusion
  727.8 66.5 %reduce-scatter.4.cloned.1.call-done = f32[8192,128]{1,0:T(8,128)} async-done(((f32[32768,128]{1,0:T(8,128)}), f32[8192,128]{1,0:T(8,128)}) %reduce-scatter.4.cloned.1.call-update) | async-done | bytes 4194320 | tf_op jit(solution)/shard_map/reduce_scatter | solution.py:410
  794.4 2.4 convert_element_type.25
  796.8 2.6 convert_element_type.26
  (33 shorter events, 9.4 us)
Async XLA Ops:
  7.2 177.1 %all-gather.9.cloned.1.call-start = ((), (), s32[]{:S(2)}) async-start(), calls=%async_computation.10 | async-start | bytes 10485760 | tf_op jit(solution)/shard_map/all_gather | solution.py:407
  7.9 176.4 %all-gather.5.cloned.1.call-start = ((), (), s32[]{:S(2)}) async-start(), calls=%async_computation.5 | async-start | bytes 10485760 | tf_op jit(solution)/shard_map/all_gather | solution.py:407
  7.9 107.1 %collective-permute-start = (bf16[2048,512]{1,0:T(8,128)(2,1)}, bf16[2048,512]{1,0:T(8,128)(2,1)S(1)}, u32[]{:S(2)}, u32[]{:S(2)}) collective-permute-start(bf16[2048,512]{1,0:T(8,128)(2,1)} %bitcast.31), channel_id=1, source_target_pairs={{0,4},{4,0},{1,5},{5,1},{2,6},{6,2},{3,7},{7,3}} | collective-permute-start | bytes 6291464 | tf_op jit(solution)/shard_map/ppermute | solution.py:421
  11.3 47.9 %collective-permute-start.2 = (f32[2048,8]{0,1:T(8,128)}, f32[2048,8]{0,1:T(8,128)S(1)}, u32[]{:S(2)}, u32[]{:S(2)}) collective-permute-start(f32[2048,8]{0,1:T(8,128)} %bitcast.33), channel_id=1, source_target_pairs={{0,4},{4,0},{1,5},{5,1},{2,6},{6,2},{3,7},{7,3}} | collective-permute-start | bytes 196616 | tf_op jit(solution)/shard_map/ppermute | solution.py:420
  11.3 49.3 %collective-permute-start.1 = (s32[2048,8]{0,1:T(8,128)}, s32[2048,8]{0,1:T(8,128)S(1)}, u32[]{:S(2)}, u32[]{:S(2)}) collective-permute-start(s32[2048,8]{0,1:T(8,128)} %bitcast.34), channel_id=1, source_target_pairs={{0,4},{4,0},{1,5},{5,1},{2,6},{6,2},{3,7},{7,3}} | collective-permute-start | bytes 196616 | tf_op jit(solution)/shard_map/ppermute | solution.py:419
  115.1 1.3 copy-start
  116.4 67.9 %collective-permute-start.3 = (bf16[2048,512]{1,0:T(8,128)(2,1)}, bf16[2048,512]{1,0:T(8,128)(2,1)S(1)}, u32[]{:S(2)}, u32[]{:S(2)}) collective-permute-start(bf16[2048,512]{1,0:T(8,128)(2,1)} %bitcast.32), channel_id=1, source_target_pairs={{0,4},{4,0},{1,5},{5,1},{2,6},{6,2},{3,7},{7,3}} | collective-permute-start | bytes 6291464 | tf_op jit(solution)/shard_map/ppermute | solution.py:429
  118.2 57.5 %all-to-all-start = ((s32[4,1,8448]{2,1,0:T(1,128)}), s32[4,1,8448]{2,1,0:T(1,128)S(1)}, u32[]{:S(2)}, u32[]{:S(2)}) async-start(s32[4,1,8448]{2,1,0:T(1,128)} %bitcast.22), calls=%async_computation | async-start | bytes 270336 | tf_op jit(solution)/shard_map/all_to_all | solution.py:416
  175.6 8.0 all-to-all-start.1
  179.0 138.0 %all-gather.7.cloned.1.call-start = ((), (), s32[]{:S(2)}) async-start(), calls=%async_computation.6 | async-start | bytes 10485760 | tf_op jit(solution)/shard_map/all_gather | solution.py:407
  184.3 1.3 copy-start.1
  185.6 418.6 %reduce-scatter.6.cloned.1.call-start = ((), (), s32[]{:S(2)}) async-start(), calls=%async_computation.8 | async-start | bytes 10485760 | tf_op jit(solution)/shard_map/reduce_scatter | solution.py:410
  503.7 168.8 %reduce-scatter.8.cloned.1.call-start = ((), (), s32[]{:S(2)}) async-start(), calls=%async_computation.9 | async-start | bytes 10485760 | tf_op jit(solution)/shard_map/reduce_scatter | solution.py:410
  504.3 290.1 %reduce-scatter.4.cloned.1.call-start = ((), (), s32[]{:S(2)}) async-start(), calls=%async_computation.7 | async-start | bytes 20971520 | tf_op jit(solution)/shard_map/reduce_scatter | solution.py:410
  675.6 49.2 %collective-permute-start.5 = (bf16[1024,512]{1,0:T(8,128)(2,1)}, bf16[1024,512]{1,0:T(8,128)(2,1)}, u32[]{:S(2)}, u32[]{:S(2)}) collective-permute-start(bf16[1024,512]{1,0:T(8,128)(2,1)} %convert_element_type.30), channel_id=1, source_target_pairs={{4,0},{0,4},{5,1},{1,5},{6,2},{2,6},{7,3},{3,7}} | collective-permute-start | bytes 3145736 | tf_op jit(solution)/shard_map/ppermute | solution.py:443
  677.1 47.8 %collective-permute-start.4 = (bf16[1024,512]{1,0:T(8,128)(2,1)}, bf16[1024,512]{1,0:T(8,128)(2,1)}, u32[]{:S(2)}, u32[]{:S(2)}) collective-permute-start(bf16[1024,512]{1,0:T(8,128)(2,1)} %convert_element_type.28), channel_id=1, source_target_pairs={{4,0},{0,4},{5,1},{1,5},{6,2},{2,6},{7,3},{3,7}} | collective-permute-start | bytes 3145736 | tf_op jit(solution)/shard_map/ppermute | solution.py:442
Sparse Core Ops, SparseCore 0:
  9.5 58.2 all-gather.8
  116.5 56.6 all-gather.4
  185.7 54.3 all-gather.6
  503.8 100.3 reduce-scatter.5
  606.6 65.8 reduce-scatter.7
  674.9 119.4 reduce-scatter.3

commit v4 on v3

--- a/solution.py
+++ b/solution.py
@@ -17,6 +17,7 @@
 TILE_GROUPS = TILE // GROUP
 LANES = 128
 SUB = 4
+FFN_STEP = 256
 STAGE_ROWS = 128
 STAGE_SLOTS = 8
 VMEM_LIMIT = 66 * 1000 * 1000
@@ -193,8 +194,8 @@
         coming = jnp.where(i + 1 < tiles, here + (i + 1) * TILE_GROUPS, following)
 
         def side(part, parts):
-            per = TILE_GROUPS // parts
-            for q in range(part * per, (part + 1) * per, 2):
+            pairs = TILE_GROUPS // 2
+            for q in range(2 * (part * pairs // parts), 2 * ((part + 1) * pairs // parts), 2):
                 add_groups(tok, g, acc, out_buf, [grp[last + q], grp[last + q + 1]], q * GROUP, n_col)
                 for r in (q, q + 1):
                     pick_group(tok, g, tables, pick_bufs, grp[coming + r], r * GROUP, n_col)
@@ -229,14 +230,14 @@
         rows = pl.ds(pl.multiple_of(i * TILE, TILE), TILE)
         x = tile_rows(x_buf, n_col)
         d_ref[0, rows, :] = tile_rows(d_buf, n_col)
-        side(0, 4)
-        pre_one = dot_nn(x, w_one[0])
-        side(1, 4)
-        pre_three = dot_nn(x, w_three[0])
-        side(2, 4)
-        hidden = (pre_one * jax.nn.sigmoid(pre_one) * pre_three).astype(BF16)
-        side(3, 4)
-        put_rows(out_buf, dot_nn(hidden, w_two[0]).astype(BF16), n_col)
+        ffn = w_one.shape[2]
+        hidden = []
+        for k, f in enumerate(range(0, ffn, FFN_STEP)):
+            side(k, ffn // FFN_STEP + 0)
+            pre_one = dot_nn(x, w_one[0, :, f:f + FFN_STEP])
+            pre_three = dot_nn(x, w_three[0, :, f:f + FFN_STEP])
+            hidden.append((pre_one * jax.nn.sigmoid(pre_one) * pre_three).astype(BF16))
+        put_rows(out_buf, dot_nn(jnp.concatenate(hidden, axis=1), w_two[0]).astype(BF16), n_col)
 
     pipelined_tiles(e, n_src, n_local, n_col, tok, g, grp, prev, (x_table, d_table), (x_buf, d_buf), acc, out_buf, compute)
 
@@ -302,21 +303,20 @@
         rows = pl.ds(pl.multiple_of(i * TILE, TILE), TILE)
         x = tile_rows(x_buf, n_col)
         x_ref[0, rows, :] = x
-        side(0, 4)
-        pre_one = dot_nn(x, w_one[0])
-        side(1, 4)
-        pre_three = dot_nn(x, w_three[0])
-        side(2, 4)
-        d_hidden = dot_nt(d_ref[0, rows, :], w_two[0]).astype(BF16).astype(F32)
-        side(3, 4)
-        sig_one = jax.nn.sigmoid(pre_one)
-        act_one = pre_one * sig_one
-        h_ref[0, rows, :] = (act_one * pre_three).astype(BF16)
-        d_three = (d_hidden * act_one).astype(BF16)
-        d_one = (d_hidden * pre_three * sig_one * (1.0 + pre_one * (1.0 - sig_one))).astype(BF16)
-        d1_ref[0, rows, :] = d_one
-        d3_ref[0, rows, :] = d_three
-        dx = dot_nt(d_one, w_one[0]) + dot_nt(d_three, w_three[0])
+        d = d_ref[0, rows, :]
+        ffn = w_one.shape[2]
+        for k, f in enumerate(range(0, ffn, FFN_STEP)):
+            cols = slice(f, f + FFN_STEP)
+            side(k, ffn // FFN_STEP + 0)
+            pre_one = dot_nn(x, w_one[0, :, cols])
+            pre_three = dot_nn(x, w_three[0, :, cols])
+            d_hidden = dot_nt(d, w_two[0, cols, :]).astype(BF16).astype(F32)
+            sig_one = jax.nn.sigmoid(pre_one)
+            act_one = pre_one * sig_one
+            h_ref[0, rows, cols] = (act_one * pre_three).astype(BF16)
+            d3_ref[0, rows, cols] = (d_hidden * act_one).astype(BF16)
+            d1_ref[0, rows, cols] = (d_hidden * pre_three * sig_one * (1.0 + pre_one * (1.0 - sig_one))).astype(BF16)
+        dx = dot_nt(d1_ref[0, rows, :], w_one[0]) + dot_nt(d3_ref[0, rows, :], w_three[0])
         put_rows(out_buf, dx.astype(BF16), n_col)
 
     pipelined_tiles(e, n_src, n_local, n_col, tok, None, grp, prev, (table,), (x_buf,), acc, out_buf, compute)
@@ -418,7 +418,8 @@
 
         idx_dst = lax.ppermute(route_idx[0], 'stage', to_next)
         wts_dst = lax.ppermute(route_wts[0], 'stage', to_next)
-        x_dst = lax.ppermute(x_act[0], 'stage', to_next)
+        idx_dst, wts_dst, x_src = lax.optimization_barrier((idx_dst, wts_dst, x_act[0]))
+        x_dst = lax.ppermute(x_src, 'stage', to_next)
         dy_all = gather_tokens(dy_act[0])
         idx_dst = idx_dst.reshape(-1)
         wts_dst = wts_dst.reshape(-1)

time: 808 us -> 747 us (0.925)
  waiting for transfers between devices: 215 us -> 168 us
  Pallas kernels: 540 us -> 528 us
    ppermute x1, waiting for transfers between devices: 45.9 us -> 1.93 us  [moe_body(): wts_dst = lax.ppermute(route_wts[0], 'stage', to_next)]
    pallas_call x1, Pallas kernels: 187 us -> 178 us  [backward_partial(): pl.pallas_call(functools.partial(backward_kernel, n_src, n_local, n_rows,...]
  transfers between devices with their start and end apart: 14 -> 14, of which waited for: 5 -> 6; matrix products, arithmetic and copies ran while one was open for 2% -> 2% of each run, Pallas kernels for 44% -> 47%
where the time goes in v4:
time: 747 us; the launch traced here: 746 us
  Pallas kernels  528 us (71%)
  waiting for transfers between devices  168 us (22%)
  starting transfers between devices  14.4 us (2%)
  between operations  14.2 us (2%)
  local copies, waits for them, and re-layouts  12.2 us (2%)
  other arithmetic  8.77 us (1%)
    pallas_call x1, Pallas kernels, backward_partial(): pl.pallas_call(functools.partial(backward_kernel, n_src, n_local, n_rows,...  178 us
    reduce_scatter x3, waiting for transfers between devices, scatter_sums(): own = lax.psum_scatter(partial, 'expert', scatter_dimension=0, tiled=True)  158 us
    pallas_call x1, Pallas kernels, forward_partial(): pl.pallas_call(functools.partial(forward_kernel, n_src, n_local, n_rows,...  126 us
    pallas_call x2, Pallas kernels, weight_grads(): pl.pallas_call(functools.partial(grad_kernel, n_src, first), out_shape=(i...  117 us
    pallas_call x2, Pallas kernels, route_lists(): pl.pallas_call(functools.partial(route_kernel, n_tok, n_pair // n_tok, n_...  107 us
  transfers between devices with their start and end apart: 14, of which 6 were waited for; matrix products, arithmetic and copies ran while one was open for 2% of the time, Pallas kernels for 47%

profile of v4, /device:TPU:0, one launch (start us, length us, event | category | flops | bytes accessed | tf_op | source)
XLA Modules:
  0.0 745.8 jit_solution(12865874315687586819)
XLA Ops:
  7.9 3.4 collective-permute-start
  11.3 2.5 collective-permute-done
  13.9 1.9 collective-permute-done.1
  19.6 53.0 %route_lists.2 = s32[33792]{0:T(1024)} custom-call(s32[16384]{0:T(1024)} %reshape.51.idx_ref, s32[1]{0:T(128)} %bitcast.3.val_ref), custom_call_target="tpu_custom_call" | custom-call | flops 4000000000 | bytes 270336 | tf_op jit(solution)/shard_map/route_lists/pallas_call | solution.py:69
  72.6 1.3 copy-done
  75.0 3.3 all-to-all-start
  78.3 54.1 %route_lists.3 = f32[33792]{0:T(1024)} custom-call(s32[16384]{0:T(1024)} %reshape.51.idx_ref, f32[16384]{0:T(1024)} %reshape.53.val_ref), custom_call_target="tpu_custom_call" | custom-call | flops 4000000000 | bytes 270336 | tf_op jit(solution)/shard_map/route_lists/pallas_call | solution.py:69
  132.5 3.3 all-to-all-start.1
  136.5 3.9 all-to-all-done.1
  142.5 126.3 %forward_partial.1 = (f32[32768,128]{1,0:T(8,128)}, bf16[32,1024,512]{2,1,0:T(8,128)(2,1)}, s32[32]{0:T(128)}) custom-call(s32[33920]{0:T(1024)} %concatenate.9.tok_hbm, f32[33920]{0:T(1024)} %concatenate.10.g_hbm, bf16[8192,512]{1,0:T(8,128)(2,1)} %all-gather.5.cloned.1.call-done.x_hbm, bf16[8192,512]{1,0:T(8,128)(2,1)} %bitcast.30, ...), custom_call_target="tpu_custom_call" | custom-call | flops 38654705664 | bytes 75497472 | tf_op jit(solution)/shard_map/forward_partial/pallas_call | solution.py:276
  268.8 178.0 %backward_partial.1 = (f32[16384,128]{1,0:T(8,128)}, f32[16384,128]{1,0:T(8,128)}, bf16[32,1024,512]{2,1,0:T(8,128)(2,1)}, bf16[32,1024,768]{2,1,0:T(8,128)(2,1)...) custom-call(s32[33920]{0:T(1024)} %concatenate.9.tok_hbm, ...), custom_call_target="tpu_custom_call" | custom-call | flops 64424509440 | bytes 150994944 | tf_op jit(solution)/shard_map/backward_partial/pallas_call | solution.py:346
  448.0 69.6 %weight_grads.2 = (bf16[32,512,768]{2,1,0:T(8,128)(2,1)}, bf16[32,512,768]{2,1,0:T(8,128)(2,1)}, bf16[32,768,512]{2,1,0:T(8,128)(2,1)}) custom-call(s32[32]{0:T(128)} %get-tuple-element.56.tiles, bf16[32,1024,512]{2,1,0:T(8,128)(2,1)} %get-tuple-element.57.x_ref, bf16[32,1024,512]{2,1,0:T(8,128)(2,1)} %get-tuple-element.53.d_ref, ...), custom_call_target="tpu_custom_call" | custom-call | flops 24159191040 | bytes 94371840 | tf_op jit(solution)/shard_map/weight_grads/pallas_call | solution.py:378
  517.6 26.2 %reduce-scatter.6.cloned.1.call-done = f32[4096,128]{1,0:T(8,128)} async-done(((f32[16384,128]{1,0:T(8,128)}), f32[4096,128]{1,0:T(8,128)}) %reduce-scatter.6.cloned.1.call-update) | async-done | bytes 2097168 | tf_op jit(solution)/shard_map/reduce_scatter | solution.py:410
  543.8 1.7 convert_element_type.27
  545.5 1.4 convert_element_type.28
  546.9 65.1 %reduce-scatter.8.cloned.1.call-done = f32[4096,128]{1,0:T(8,128)} async-done(((f32[16384,128]{1,0:T(8,128)}), f32[4096,128]{1,0:T(8,128)}) %reduce-scatter.8.cloned.1.call-update) | async-done | bytes 2097168 | tf_op jit(solution)/shard_map/reduce_scatter | solution.py:410
  612.1 1.7 convert_element_type.29
  613.8 1.4 convert_element_type.30
  615.2 1.5 collective-permute-start.5
  617.2 47.2 %weight_grads.3 = (bf16[32,512,768]{2,1,0:T(8,128)(2,1)}, bf16[32,512,768]{2,1,0:T(8,128)(2,1)}, bf16[32,768,512]{2,1,0:T(8,128)(2,1)}) custom-call(s32[32]{0:T(128)} %get-tuple-element.56.tiles, bf16[32,1024,512]{2,1,0:T(8,128)(2,1)} %get-tuple-element.57.x_ref, ...), custom_call_target="tpu_custom_call", output_to_operand_aliasing={{0}: (6, {}), {1}: (7, {}), {2}: (8, {})} | custom-call | flops 14495514624 | bytes 56623104 | tf_op jit(solution)/shard_map/weight_grads/pallas_call | solution.py:378
  664.4 3.0 maximum_bitcast_fusion
  667.4 66.5 %reduce-scatter.4.cloned.1.call-done = f32[8192,128]{1,0:T(8,128)} async-done(((f32[32768,128]{1,0:T(8,128)}), f32[8192,128]{1,0:T(8,128)}) %reduce-scatter.4.cloned.1.call-update) | async-done | bytes 4194320 | tf_op jit(solution)/shard_map/reduce_scatter | solution.py:410
  734.0 2.4 convert_element_type.25
  736.4 2.6 convert_element_type.26
  (33 shorter events, 10.2 us)
Async XLA Ops:
  7.2 133.9 %all-gather.9.cloned.1.call-start = ((), (), s32[]{:S(2)}) async-start(), calls=%async_computation.10 | async-start | bytes 10485760 | tf_op jit(solution)/shard_map/all_gather | solution.py:407
  7.9 133.2 %all-gather.5.cloned.1.call-start = ((), (), s32[]{:S(2)}) async-start(), calls=%async_computation.5 | async-start | bytes 10485760 | tf_op jit(solution)/shard_map/all_gather | solution.py:407
  7.9 5.9 collective-permute-start
  11.3 4.5 collective-permute-start.1
  15.8 56.8 %collective-permute-start.2 = (bf16[2048,512]{1,0:T(8,128)(2,1)}, bf16[2048,512]{1,0:T(8,128)(2,1)S(1)}, u32[]{:S(2)}, u32[]{:S(2)}) collective-permute-start(bf16[2048,512]{1,0:T(8,128)(2,1)} %bitcast.31), channel_id=1, source_target_pairs={{0,4},{4,0},{1,5},{5,1},{2,6},{6,2},{3,7},{7,3}} | collective-permute-start | bytes 6291464 | tf_op jit(solution)/shard_map/ppermute | solution.py:422
  72.6 1.3 copy-start
  73.9 67.2 %collective-permute-start.3 = (bf16[2048,512]{1,0:T(8,128)(2,1)}, bf16[2048,512]{1,0:T(8,128)(2,1)S(1)}, u32[]{:S(2)}, u32[]{:S(2)}) collective-permute-start(bf16[2048,512]{1,0:T(8,128)(2,1)} %bitcast.32), channel_id=1, source_target_pairs={{0,4},{4,0},{1,5},{5,1},{2,6},{6,2},{3,7},{7,3}} | collective-permute-start | bytes 6291464 | tf_op jit(solution)/shard_map/ppermute | solution.py:430
  75.0 57.5 %all-to-all-start = ((s32[4,1,8448]{2,1,0:T(1,128)}), s32[4,1,8448]{2,1,0:T(1,128)S(1)}, u32[]{:S(2)}, u32[]{:S(2)}) async-start(s32[4,1,8448]{2,1,0:T(1,128)} %bitcast.22), calls=%async_computation | async-start | bytes 270336 | tf_op jit(solution)/shard_map/all_to_all | solution.py:416
  132.5 8.0 %all-to-all-start.1 = ((f32[4,1,8448]{2,1,0:T(1,128)}), f32[4,1,8448]{2,1,0:T(1,128)S(1)}, u32[]{:S(2)}, u32[]{:S(2)}) async-start(f32[4,1,8448]{2,1,0:T(1,128)} %bitcast.23), calls=%async_computation.1 | async-start | bytes 270336 | tf_op jit(solution)/shard_map/all_to_all | solution.py:416
  135.8 133.0 %all-gather.7.cloned.1.call-start = ((), (), s32[]{:S(2)}) async-start(), calls=%async_computation.6 | async-start | bytes 10485760 | tf_op jit(solution)/shard_map/all_gather | solution.py:407
  141.1 1.3 copy-start.1
  142.4 401.3 %reduce-scatter.6.cloned.1.call-start = ((), (), s32[]{:S(2)}) async-start(), calls=%async_computation.8 | async-start | bytes 10485760 | tf_op jit(solution)/shard_map/reduce_scatter | solution.py:410
  446.9 165.2 %reduce-scatter.8.cloned.1.call-start = ((), (), s32[]{:S(2)}) async-start(), calls=%async_computation.9 | async-start | bytes 10485760 | tf_op jit(solution)/shard_map/reduce_scatter | solution.py:410
  447.4 286.5 %reduce-scatter.4.cloned.1.call-start = ((), (), s32[]{:S(2)}) async-start(), calls=%async_computation.7 | async-start | bytes 20971520 | tf_op jit(solution)/shard_map/reduce_scatter | solution.py:410
  615.2 49.2 %collective-permute-start.5 = (bf16[1024,512]{1,0:T(8,128)(2,1)}, bf16[1024,512]{1,0:T(8,128)(2,1)}, u32[]{:S(2)}, u32[]{:S(2)}) collective-permute-start(bf16[1024,512]{1,0:T(8,128)(2,1)} %convert_element_type.30), channel_id=1, source_target_pairs={{4,0},{0,4},{5,1},{1,5},{6,2},{2,6},{7,3},{3,7}} | collective-permute-start | bytes 3145736 | tf_op jit(solution)/shard_map/ppermute | solution.py:444
  616.7 47.8 %collective-permute-start.4 = (bf16[1024,512]{1,0:T(8,128)(2,1)}, bf16[1024,512]{1,0:T(8,128)(2,1)}, u32[]{:S(2)}, u32[]{:S(2)}) collective-permute-start(bf16[1024,512]{1,0:T(8,128)(2,1)} %convert_element_type.28), channel_id=1, source_target_pairs={{4,0},{0,4},{5,1},{1,5},{6,2},{2,6},{7,3},{3,7}} | collective-permute-start | bytes 3145736 | tf_op jit(solution)/shard_map/ppermute | solution.py:443
Sparse Core Ops, SparseCore 0:
  9.5 58.2 all-gather.8
  74.0 55.9 all-gather.4
  142.6 54.9 all-gather.6
  447.0 96.7 reduce-scatter.5
  546.2 65.8 reduce-scatter.7
  614.5 119.4 reduce-scatter.3

commit v5 on v4

--- a/solution.py
+++ b/solution.py
@@ -151,16 +151,16 @@
             bufs[1][dst, :] = tables[1][src, :] * g[base + k]
 
 
-def add_groups(tok, g, acc, buf, bases, row, n_col):
-    dsts, rows = [], []
-    for q, base in enumerate(bases):
-        for k in range(GROUP):
+def add_group(tok, g, acc, buf, base, row, n_col, step):
+    for first in range(0, GROUP, step):
+        dsts, rows = [], []
+        for k in range(first, first + step):
             dsts.append(rows_at(tok[base + k], n_col))
-            val = buf[pl.ds((row + q * GROUP + k) * n_col, n_col), :]
+            val = buf[pl.ds((row + k) * n_col, n_col), :]
             rows.append(val if g is None else val * g[base + k])
-    sums = [acc[d, :] + r for d, r in zip(dsts, rows)]
-    for d, r in zip(dsts, sums):
-        acc[d, :] = r
+        sums = [acc[d, :] + r for d, r in zip(dsts, rows)]
+        for d, r in zip(dsts, sums):
+            acc[d, :] = r
 
 
 def tile_rows(buf, n_col):
@@ -172,7 +172,7 @@
         buf[pl.ds(c, TILE, stride=n_col), :] = rows[:, c * LANES:(c + 1) * LANES].astype(F32)
 
 
-def pipelined_tiles(e, n_src, n_local, n_col, tok, g, grp, prev, tables, pick_bufs, acc, out_buf, compute):
+def pipelined_tiles(e, n_src, n_local, n_col, tok, g, grp, prev, tables, pick_bufs, acc, out_buf, step, compute):
     tiles = n_tiles(tok, e, n_src, n_local)
     here = lax.rem(e, 3) * SLOT
     following = lax.rem(e + 1, 3) * SLOT
@@ -194,11 +194,9 @@
         coming = jnp.where(i + 1 < tiles, here + (i + 1) * TILE_GROUPS, following)
 
         def side(part, parts):
-            pairs = TILE_GROUPS // 2
-            for q in range(2 * (part * pairs // parts), 2 * ((part + 1) * pairs // parts), 2):
-                add_groups(tok, g, acc, out_buf, [grp[last + q], grp[last + q + 1]], q * GROUP, n_col)
-                for r in (q, q + 1):
-                    pick_group(tok, g, tables, pick_bufs, grp[coming + r], r * GROUP, n_col)
+            for q in range(part * TILE_GROUPS // parts, (part + 1) * TILE_GROUPS // parts):
+                add_group(tok, g, acc, out_buf, grp[last + q], q * GROUP, n_col, step)
+                pick_group(tok, g, tables, pick_bufs, grp[coming + q], q * GROUP, n_col)
 
         compute(i, side)
         prev[0] = here + i * TILE_GROUPS
@@ -207,7 +205,7 @@
     def _():
         @pl.loop(0, TILE_GROUPS)
         def _(q):
-            add_groups(tok, g, acc, out_buf, [grp[prev[0] + q]], pl.multiple_of(q * GROUP, GROUP), n_col)
+            add_group(tok, g, acc, out_buf, grp[prev[0] + q], pl.multiple_of(q * GROUP, GROUP), n_col, step)
 
 
 def forward_kernel(n_src, n_local, n_rows, n_col, tok_hbm, g_hbm, x_hbm, dy_hbm, w_one, w_three, w_two, y_hbm, d_ref, tiles_ref, x_table, d_table, acc, x_buf, d_buf, out_buf, stage, grp, prev, sem, list_sem, tok, g):
@@ -233,13 +231,13 @@
         ffn = w_one.shape[2]
         hidden = []
         for k, f in enumerate(range(0, ffn, FFN_STEP)):
-            side(k, ffn // FFN_STEP + 0)
+            side(k, ffn // FFN_STEP)
             pre_one = dot_nn(x, w_one[0, :, f:f + FFN_STEP])
             pre_three = dot_nn(x, w_three[0, :, f:f + FFN_STEP])
             hidden.append((pre_one * jax.nn.sigmoid(pre_one) * pre_three).astype(BF16))
         put_rows(out_buf, dot_nn(jnp.concatenate(hidden, axis=1), w_two[0]).astype(BF16), n_col)
 
-    pipelined_tiles(e, n_src, n_local, n_col, tok, g, grp, prev, (x_table, d_table), (x_buf, d_buf), acc, out_buf, compute)
+    pipelined_tiles(e, n_src, n_local, n_col, tok, g, grp, prev, (x_table, d_table), (x_buf, d_buf), acc, out_buf, GROUP, compute)
 
     @pl.when(e == n_local - 1)
     def _():
@@ -286,7 +284,8 @@
     )(tok, g, x_all, dy_all, w_one, w_three, w_two)
 
 
-def backward_kernel(n_src, n_local, n_rows, n_col, n_part, tok_hbm, x_hbm, d_ref, w_one, w_three, w_two, *rest):
+def backward_kernel(n_src, n_local, n_rows, n_col, cuts, tok_hbm, x_hbm, d_ref, w_one, w_three, w_two, *rest):
+    n_part = len(cuts) - 1
     parts, rest = rest[:n_part], rest[n_part:]
     x_ref, h_ref, d1_ref, d3_ref, table, acc, x_buf, out_buf, stage, grp, prev, sem, list_sem, tok = rest
     e = pl.program_id(0)
@@ -307,7 +306,7 @@
         ffn = w_one.shape[2]
         for k, f in enumerate(range(0, ffn, FFN_STEP)):
             cols = slice(f, f + FFN_STEP)
-            side(k, ffn // FFN_STEP + 0)
+            side(k, ffn // FFN_STEP)
             pre_one = dot_nn(x, w_one[0, :, cols])
             pre_three = dot_nn(x, w_three[0, :, cols])
             d_hidden = dot_nt(d, w_two[0, cols, :]).astype(BF16).astype(F32)
@@ -319,23 +318,22 @@
         dx = dot_nt(d1_ref[0, rows, :], w_one[0]) + dot_nt(d3_ref[0, rows, :], w_three[0])
         put_rows(out_buf, dx.astype(BF16), n_col)
 
-    pipelined_tiles(e, n_src, n_local, n_col, tok, None, grp, prev, (table,), (x_buf,), acc, out_buf, compute)
+    pipelined_tiles(e, n_src, n_local, n_col, tok, None, grp, prev, (table,), (x_buf,), acc, out_buf, GROUP // 2, compute)
 
     @pl.when(e == n_local - 1)
     def _():
         own = n_rows * n_col // n_src
-        part = own // n_part
-        outs = [
-            pltpu.make_async_copy(acc.at[pl.ds(q * own + k * part, part)], parts[k].at[pl.ds(q * part, part)], sem.at[0])
-            for k in range(n_part) for q in range(n_src)
-        ]
+        outs = []
+        for k, (lo, hi) in enumerate(zip(cuts, cuts[1:])):
+            part = (hi - lo) * n_col
+            outs += [pltpu.make_async_copy(acc.at[pl.ds(q * own + lo * n_col, part)], parts[k].at[pl.ds(q * part, part)], sem.at[0]) for q in range(n_src)]
         for out in outs:
             out.start()
         for out in outs:
             out.wait()
 
 
-def backward_partial(tok, x_all, d_rows, w_one, w_three, w_two, n_src, n_part):
+def backward_partial(tok, x_all, d_rows, w_one, w_three, w_two, n_src, cuts):
     n_rows, model = x_all.shape
     n_local, cap, _ = d_rows.shape
     ffn = w_one.shape[2]
@@ -343,9 +341,10 @@
     hbm = pl.BlockSpec(memory_space=pl.ANY)
     ffn_out = jax.ShapeDtypeStruct((n_local, cap, ffn), BF16)
     pairs = n_rows * 8 // n_src
+    n_part = len(cuts) - 1
     outs = pl.pallas_call(
-        functools.partial(backward_kernel, n_src, n_local, n_rows, n_col, n_part),
-        out_shape=(jax.ShapeDtypeStruct((n_rows * n_col // n_part, LANES), F32),) * n_part + (jax.ShapeDtypeStruct((n_local, cap, model), BF16), ffn_out, ffn_out, ffn_out),
+        functools.partial(backward_kernel, n_src, n_local, n_rows, n_col, cuts),
+        out_shape=tuple(jax.ShapeDtypeStruct((n_src * (hi - lo) * n_col, LANES), F32) for lo, hi in zip(cuts, cuts[1:])) + (jax.ShapeDtypeStruct((n_local, cap, model), BF16), ffn_out, ffn_out, ffn_out),
         grid=(n_local,),
         in_specs=[hbm, hbm, per_expert(cap, model), per_expert(model, ffn), per_expert(model, ffn), per_expert(ffn, model)],
         out_specs=(hbm,) * n_part + (per_expert(cap, model), per_expert(cap, ffn), per_expert(cap, ffn), per_expert(cap, ffn)),
@@ -437,12 +436,12 @@
         y_sum, x_all_again, d_rows = lax.optimization_barrier((y_sum, x_all_again, d_rows))
         y_dst = scatter_sums(y_sum)
 
-        (dx_low, dx_high), (x_rows, hidden, d_one, d_three) = backward_partial(tok, x_all_again, d_rows, w_in_one, w_in_three, w_out, n_dev, 2)
+        (dx_low, dx_high), (x_rows, hidden, d_one, d_three) = backward_partial(tok, x_all_again, d_rows, w_in_one, w_in_three, w_out, n_dev, (0, n_tok * 3 // 4, n_tok))
         dx_low = scatter_sums(dx_low)
         dx_high = scatter_sums(dx_high)
         dx_low = lax.ppermute(dx_low, 'stage', to_prev)
         dx_high = lax.ppermute(dx_high, 'stage', to_prev)
-        early = n_local * 5 // 8
+        early = n_local * 7 // 8
         grads = weight_grads(tiles, x_rows, d_rows, hidden, d_one, d_three, n_dev, 0, early, ())
         g_one, g_three, g_two = weight_grads(tiles, x_rows, d_rows, hidden, d_one, d_three, n_dev, early, n_local - early, grads)
         dx_src = jnp.concatenate([dx_low, dx_high])

time: 747 us -> 732 us (0.980)
  Pallas kernels: 528 us -> 512 us
    pallas_call x1, Pallas kernels: 178 us -> 169 us  [backward_partial(): pl.pallas_call(functools.partial(backward_kernel, n_src, n_local, n_rows,...]
  transfers between devices with their start and end apart: 14 -> 14, of which waited for: 6 -> 5; matrix products, arithmetic and copies ran while one was open for 2% -> 2% of each run, Pallas kernels for 47% -> 47%
where the time goes in v5:
time: 732 us; the launch traced here: 731 us
  Pallas kernels  512 us (70%)
  waiting for transfers between devices  168 us (23%)
  starting transfers between devices  15.3 us (2%)
  between operations  14.3 us (2%)
  local copies, waits for them, and re-layouts  12 us (2%)
  other arithmetic  8.74 us (1%)
    pallas_call x1, Pallas kernels, backward_partial(): pl.pallas_call(functools.partial(backward_kernel, n_src, n_local, n_rows,...  169 us
    reduce_scatter x3, waiting for transfers between devices, scatter_sums(): own = lax.psum_scatter(partial, 'expert', scatter_dimension=0, tiled=True)  158 us
    pallas_call x1, Pallas kernels, forward_partial(): pl.pallas_call(functools.partial(forward_kernel, n_src, n_local, n_rows,...  119 us
    pallas_call x2, Pallas kernels, weight_grads(): pl.pallas_call(functools.partial(grad_kernel, n_src, first), out_shape=(i...  117 us
    pallas_call x2, Pallas kernels, route_lists(): pl.pallas_call(functools.partial(route_kernel, n_tok, n_pair // n_tok, n_...  107 us
  transfers between devices with their start and end apart: 14, of which 5 were waited for; matrix products, arithmetic and copies ran while one was open for 2% of the time, Pallas kernels for 47%

profile of v5, /device:TPU:0, one launch (start us, length us, event | category | flops | bytes accessed | tf_op | source)
XLA Modules:
  0.0 730.9 jit_solution(10911670860457781051)
XLA Ops:
  7.9 3.4 collective-permute-start
  11.3 2.5 collective-permute-done
  13.9 1.9 collective-permute-done.1
  19.6 53.0 %route_lists.2 = s32[33792]{0:T(1024)} custom-call(s32[16384]{0:T(1024)} %reshape.51.idx_ref, s32[1]{0:T(128)} %bitcast.3.val_ref), custom_call_target="tpu_custom_call" | custom-call | flops 4000000000 | bytes 270336 | tf_op jit(solution)/shard_map/route_lists/pallas_call | solution.py:69
  72.6 1.3 copy-done
  75.0 3.3 all-to-all-start
  78.3 54.1 %route_lists.3 = f32[33792]{0:T(1024)} custom-call(s32[16384]{0:T(1024)} %reshape.51.idx_ref, f32[16384]{0:T(1024)} %reshape.53.val_ref), custom_call_target="tpu_custom_call" | custom-call | flops 4000000000 | bytes 270336 | tf_op jit(solution)/shard_map/route_lists/pallas_call | solution.py:69
  132.5 3.3 all-to-all-start.1
  136.5 3.9 all-to-all-done.1
  141.1 1.3 copy-done.1
  142.5 119.1 %forward_partial.1 = (f32[32768,128]{1,0:T(8,128)}, bf16[32,1024,512]{2,1,0:T(8,128)(2,1)}, s32[32]{0:T(128)}) custom-call(s32[33920]{0:T(1024)} %concatenate.9.tok_hbm, f32[33920]{0:T(1024)} %concatenate.10.g_hbm, bf16[8192,512]{1,0:T(8,128)(2,1)} %all-gather.5.cloned.1.call-done.x_hbm, bf16[8192,512]{1,0:T(8,128)(2,1)} %bitcast.30, ...), custom_call_target="tpu_custom_call" | custom-call | flops 38654705664 | bytes 75497472 | tf_op jit(solution)/shard_map/forward_partial/pallas_call | solution.py:274
  261.6 168.8 %backward_partial.1 = (f32[24576,128]{1,0:T(8,128)}, f32[8192,128]{1,0:T(8,128)}, bf16[32,1024,512]{2,1,0:T(8,128)(2,1)}, bf16[32,1024,768]{2,1,0:T(8,128)(2,1)}...) custom-call(s32[33920]{0:T(1024)} %concatenate.9.tok_hbm, ...), custom_call_target="tpu_custom_call" | custom-call | flops 64424509440 | bytes 150994944 | tf_op jit(solution)/shard_map/backward_partial/pallas_call | solution.py:345
  431.6 63.9 %reduce-scatter.8.cloned.1.call-done = f32[2048,128]{1,0:T(8,128)} async-done(((f32[8192,128]{1,0:T(8,128)}), f32[2048,128]{1,0:T(8,128)}) %reduce-scatter.8.cloned.1.call-update) | async-done | bytes 1048592 | tf_op jit(solution)/shard_map/reduce_scatter | solution.py:409
  495.5 1.3 convert_element_type.29
  497.1 1.5 collective-permute-start.5
  498.6 94.2 %reduce-scatter.6.cloned.1.call-done = f32[6144,128]{1,0:T(8,128)} async-done(((f32[24576,128]{1,0:T(8,128)}), f32[6144,128]{1,0:T(8,128)}) %reduce-scatter.6.cloned.1.call-update) | async-done | bytes 3145744 | tf_op jit(solution)/shard_map/reduce_scatter | solution.py:409
  592.8 2.0 convert_element_type.27
  594.8 2.4 convert_element_type.28
  597.2 1.5 collective-permute-start.4
  598.7 100.2 %weight_grads.2 = (bf16[32,512,768]{2,1,0:T(8,128)(2,1)}, bf16[32,512,768]{2,1,0:T(8,128)(2,1)}, bf16[32,768,512]{2,1,0:T(8,128)(2,1)}) custom-call(s32[32]{0:T(128)} %get-tuple-element.56.tiles, bf16[32,1024,512]{2,1,0:T(8,128)(2,1)} %get-tuple-element.57.x_ref, bf16[32,1024,512]{2,1,0:T(8,128)(2,1)} %get-tuple-element.53.d_ref, ...), custom_call_target="tpu_custom_call" | custom-call | flops 33822867456 | bytes 132120576 | tf_op jit(solution)/shard_map/weight_grads/pallas_call | solution.py:377
  698.9 17.1 %weight_grads.3 = (bf16[32,512,768]{2,1,0:T(8,128)(2,1)}, bf16[32,512,768]{2,1,0:T(8,128)(2,1)}, bf16[32,768,512]{2,1,0:T(8,128)(2,1)}) custom-call(s32[32]{0:T(128)} %get-tuple-element.56.tiles, bf16[32,1024,512]{2,1,0:T(8,128)(2,1)} %get-tuple-element.57.x_ref, ...), custom_call_target="tpu_custom_call", output_to_operand_aliasing={{0}: (6, {}), {1}: (7, {}), {2}: (8, {})} | custom-call | flops 4831838208 | bytes 18874368 | tf_op jit(solution)/shard_map/weight_grads/pallas_call | solution.py:377
  716.0 3.0 maximum_bitcast_fusion
  719.1 2.4 convert_element_type.25
  721.5 2.6 convert_element_type.26
  (33 shorter events, 8.6 us)
Async XLA Ops:
  7.2 133.9 %all-gather.9.cloned.1.call-start = ((), (), s32[]{:S(2)}) async-start(), calls=%async_computation.10 | async-start | bytes 10485760 | tf_op jit(solution)/shard_map/all_gather | solution.py:406
  7.9 133.2 %all-gather.5.cloned.1.call-start = ((), (), s32[]{:S(2)}) async-start(), calls=%async_computation.5 | async-start | bytes 10485760 | tf_op jit(solution)/shard_map/all_gather | solution.py:406
  7.9 5.9 collective-permute-start
  11.3 4.5 collective-permute-start.1
  15.8 56.8 %collective-permute-start.2 = (bf16[2048,512]{1,0:T(8,128)(2,1)}, bf16[2048,512]{1,0:T(8,128)(2,1)S(1)}, u32[]{:S(2)}, u32[]{:S(2)}) collective-permute-start(bf16[2048,512]{1,0:T(8,128)(2,1)} %bitcast.31), channel_id=1, source_target_pairs={{0,4},{4,0},{1,5},{5,1},{2,6},{6,2},{3,7},{7,3}} | collective-permute-start | bytes 6291464 | tf_op jit(solution)/shard_map/ppermute | solution.py:421
  72.6 1.3 copy-start
  73.9 67.2 %collective-permute-start.3 = (bf16[2048,512]{1,0:T(8,128)(2,1)}, bf16[2048,512]{1,0:T(8,128)(2,1)S(1)}, u32[]{:S(2)}, u32[]{:S(2)}) collective-permute-start(bf16[2048,512]{1,0:T(8,128)(2,1)} %bitcast.32), channel_id=1, source_target_pairs={{0,4},{4,0},{1,5},{5,1},{2,6},{6,2},{3,7},{7,3}} | collective-permute-start | bytes 6291464 | tf_op jit(solution)/shard_map/ppermute | solution.py:429
  75.0 57.5 %all-to-all-start = ((s32[4,1,8448]{2,1,0:T(1,128)}), s32[4,1,8448]{2,1,0:T(1,128)S(1)}, u32[]{:S(2)}, u32[]{:S(2)}) async-start(s32[4,1,8448]{2,1,0:T(1,128)} %bitcast.22), calls=%async_computation | async-start | bytes 270336 | tf_op jit(solution)/shard_map/all_to_all | solution.py:415
  132.5 8.0 %all-to-all-start.1 = ((f32[4,1,8448]{2,1,0:T(1,128)}), f32[4,1,8448]{2,1,0:T(1,128)S(1)}, u32[]{:S(2)}, u32[]{:S(2)}) async-start(f32[4,1,8448]{2,1,0:T(1,128)} %bitcast.23), calls=%async_computation.1 | async-start | bytes 270336 | tf_op jit(solution)/shard_map/all_to_all | solution.py:415
  135.8 125.8 %all-gather.7.cloned.1.call-start = ((), (), s32[]{:S(2)}) async-start(), calls=%async_computation.6 | async-start | bytes 10485760 | tf_op jit(solution)/shard_map/all_gather | solution.py:406
  141.1 1.3 copy-start.1
  142.4 353.1 %reduce-scatter.8.cloned.1.call-start = ((), (), s32[]{:S(2)}) async-start(), calls=%async_computation.9 | async-start | bytes 5242880 | tf_op jit(solution)/shard_map/reduce_scatter | solution.py:409
  430.4 162.3 %reduce-scatter.6.cloned.1.call-start = ((), (), s32[]{:S(2)}) async-start(), calls=%async_computation.8 | async-start | bytes 15728640 | tf_op jit(solution)/shard_map/reduce_scatter | solution.py:409
  431.0 288.0 %reduce-scatter.4.cloned.1.call-start = ((), (), s32[]{:S(2)}) async-start(), calls=%async_computation.7 | async-start | bytes 20971520 | tf_op jit(solution)/shard_map/reduce_scatter | solution.py:409
  497.1 218.9 %collective-permute-start.5 = (bf16[512,512]{1,0:T(8,128)(2,1)S(1)}, bf16[512,512]{1,0:T(8,128)(2,1)}, u32[]{:S(2)}, u32[]{:S(2)}) collective-permute-start(bf16[512,512]{1,0:T(8,128)(2,1)S(1)} %convert_element_type.30), channel_id=1, source_target_pairs={{4,0},{0,4},{5,1},{1,5},{6,2},{2,6},{7,3},{3,7}} | collective-permute-start | bytes 1572872 | tf_op jit(solution)/shard_map/ppermute | solution.py:443
  597.2 118.8 %collective-permute-start.4 = (bf16[1536,512]{1,0:T(8,128)(2,1)}, bf16[1536,512]{1,0:T(8,128)(2,1)}, u32[]{:S(2)}, u32[]{:S(2)}) collective-permute-start(bf16[1536,512]{1,0:T(8,128)(2,1)} %convert_element_type.28), channel_id=1, source_target_pairs={{4,0},{0,4},{5,1},{1,5},{6,2},{2,6},{7,3},{3,7}} | collective-permute-start | bytes 4718600 | tf_op jit(solution)/shard_map/ppermute | solution.py:442
Sparse Core Ops, SparseCore 0:
  9.5 58.2 all-gather.8
  74.0 55.9 all-gather.4
  142.6 54.9 all-gather.6
  430.5 64.9 reduce-scatter.7
  498.5 94.2 reduce-scatter.5
  595.2 119.4 reduce-scatter.3

commit v6 on v5

--- a/solution.py
+++ b/solution.py
@@ -112,11 +112,15 @@
     return lax.div(tok[(p * n_local + e) * LIST + LIST - 1] + (GROUP - 1), GROUP)
 
 
-def n_tiles(tok, e, n_src, n_local):
+def all_groups(tok, e, n_src, n_local):
     groups = n_groups(tok, 0, e, n_local)
     for p in range(1, n_src):
         groups = groups + n_groups(tok, p, e, n_local)
-    return lax.div(groups + (TILE_GROUPS - 1), TILE_GROUPS)
+    return groups
+
+
+def n_tiles(tok, e, n_src, n_local):
+    return lax.div(all_groups(tok, e, n_src, n_local) + (TILE_GROUPS - 1), TILE_GROUPS)
 
 
 def list_groups(tok, grp, e, n_src, n_local):
@@ -163,16 +167,17 @@
             acc[d, :] = r
 
 
-def tile_rows(buf, n_col):
-    return jnp.concatenate([buf[pl.ds(c, TILE, stride=n_col), :] for c in range(n_col)], axis=1).astype(BF16)
+def tile_rows(buf, n_col, n_rows=TILE):
+    return jnp.concatenate([buf[pl.ds(c, n_rows, stride=n_col), :] for c in range(n_col)], axis=1).astype(BF16)
 
 
 def put_rows(buf, rows, n_col):
     for c in range(n_col):
-        buf[pl.ds(c, TILE, stride=n_col), :] = rows[:, c * LANES:(c + 1) * LANES].astype(F32)
-
-
-def pipelined_tiles(e, n_src, n_local, n_col, tok, g, grp, prev, tables, pick_bufs, acc, out_buf, step, compute):
+        buf[pl.ds(c, rows.shape[0], stride=n_col), :] = rows[:, c * LANES:(c + 1) * LANES].astype(F32)
+
+
+def pipelined_tiles(e, n_src, n_local, n_col, tok, g, grp, prev, tables, pick_bufs, acc, out_buf, step, halves, compute):
+    groups = all_groups(tok, e, n_src, n_local)
     tiles = n_tiles(tok, e, n_src, n_local)
     here = lax.rem(e, 3) * SLOT
     following = lax.rem(e + 1, 3) * SLOT
@@ -198,7 +203,19 @@
                 add_group(tok, g, acc, out_buf, grp[last + q], q * GROUP, n_col, step)
                 pick_group(tok, g, tables, pick_bufs, grp[coming + q], q * GROUP, n_col)
 
-        compute(i, side)
+        if halves:
+            short = groups - i * TILE_GROUPS <= TILE_GROUPS // 2
+
+            @pl.when(short)
+            def _():
+                compute(i, TILE // 2, side)
+
+            @pl.when(jnp.logical_not(short))
+            def _():
+                compute(i, TILE, side)
+        else:
+            compute(i, TILE, side)
+
         prev[0] = here + i * TILE_GROUPS
 
     @pl.when(e == n_local - 1)
@@ -224,9 +241,9 @@
 
     tiles_ref[e] = n_tiles(tok, e, n_src, n_local)
 
-    def compute(i, side):
+    def compute(i, used, side):
         rows = pl.ds(pl.multiple_of(i * TILE, TILE), TILE)
-        x = tile_rows(x_buf, n_col)
+        x = tile_rows(x_buf, n_col, used)
         d_ref[0, rows, :] = tile_rows(d_buf, n_col)
         ffn = w_one.shape[2]
         hidden = []
@@ -237,7 +254,7 @@
             hidden.append((pre_one * jax.nn.sigmoid(pre_one) * pre_three).astype(BF16))
         put_rows(out_buf, dot_nn(jnp.concatenate(hidden, axis=1), w_two[0]).astype(BF16), n_col)
 
-    pipelined_tiles(e, n_src, n_local, n_col, tok, g, grp, prev, (x_table, d_table), (x_buf, d_buf), acc, out_buf, GROUP, compute)
+    pipelined_tiles(e, n_src, n_local, n_col, tok, g, grp, prev, (x_table, d_table), (x_buf, d_buf), acc, out_buf, GROUP, False, compute)
 
     @pl.when(e == n_local - 1)
     def _():
@@ -298,10 +315,16 @@
         load_table(x_hbm, table, stage, sem, n_rows, n_col)
         lists.wait()
 
-    def compute(i, side):
+    def compute(i, used, side):
         rows = pl.ds(pl.multiple_of(i * TILE, TILE), TILE)
         x = tile_rows(x_buf, n_col)
         x_ref[0, rows, :] = x
+        x = x[:used]
+        if used < TILE:
+            unused = pl.ds(pl.multiple_of(i * TILE + used, TILE // 2), TILE - used)
+            for ref in (h_ref, d1_ref, d3_ref):
+                ref[0, unused, :] = jnp.zeros((TILE - used, ref.shape[2]), BF16)
+        rows = pl.ds(pl.multiple_of(i * TILE, TILE), used)
         d = d_ref[0, rows, :]
         ffn = w_one.shape[2]
         for k, f in enumerate(range(0, ffn, FFN_STEP)):
@@ -318,7 +341,7 @@
         dx = dot_nt(d1_ref[0, rows, :], w_one[0]) + dot_nt(d3_ref[0, rows, :], w_three[0])
         put_rows(out_buf, dx.astype(BF16), n_col)
 
-    pipelined_tiles(e, n_src, n_local, n_col, tok, None, grp, prev, (table,), (x_buf,), acc, out_buf, GROUP // 2, compute)
+    pipelined_tiles(e, n_src, n_local, n_col, tok, None, grp, prev, (table,), (x_buf,), acc, out_buf, GROUP // 2, True, compute)
 
     @pl.when(e == n_local - 1)
     def _():

time: 732 us -> 734 us (level)
  no operation moved by 1% of the time
where the time goes in v6:
time: 734 us; the launch traced here: 732 us
  Pallas kernels  513 us (70%)
  waiting for transfers between devices  169 us (23%)
  starting transfers between devices  15.3 us (2%)
  between operations  14.2 us (2%)
  local copies, waits for them, and re-layouts  12 us (2%)
  other arithmetic  8.74 us (1%)
    pallas_call x1, Pallas kernels, backward_partial(): pl.pallas_call(functools.partial(backward_kernel, n_src, n_local, n_rows,...  169 us
    reduce_scatter x3, waiting for transfers between devices, scatter_sums(): own = lax.psum_scatter(partial, 'expert', scatter_dimension=0, tiled=True)  159 us
    pallas_call x1, Pallas kernels, forward_partial(): pl.pallas_call(functools.partial(forward_kernel, n_src, n_local, n_rows,...  119 us
    pallas_call x2, Pallas kernels, weight_grads(): pl.pallas_call(functools.partial(grad_kernel, n_src, first), out_shape=(i...  117 us
    pallas_call x2, Pallas kernels, route_lists(): pl.pallas_call(functools.partial(route_kernel, n_tok, n_pair // n_tok, n_...  107 us
  transfers between devices with their start and end apart: 14, of which 5 were waited for; matrix products, arithmetic and copies ran while one was open for 2% of the time, Pallas kernels for 47%

profile of v6, /device:TPU:0, one launch (start us, length us, event | category | flops | bytes accessed | tf_op | source)
XLA Modules:
  0.0 732.3 jit_solution(9814483572303549200)
XLA Ops:
  7.9 3.4 collective-permute-start
  11.3 2.5 collective-permute-done
  13.9 1.9 collective-permute-done.1
  19.6 53.0 %route_lists.2 = s32[33792]{0:T(1024)} custom-call(s32[16384]{0:T(1024)} %reshape.51.idx_ref, s32[1]{0:T(128)} %bitcast.3.val_ref), custom_call_target="tpu_custom_call" | custom-call | flops 4000000000 | bytes 270336 | tf_op jit(solution)/shard_map/route_lists/pallas_call | solution.py:69
  72.6 1.3 copy-done
  75.0 3.3 all-to-all-start
  78.3 54.1 %route_lists.3 = f32[33792]{0:T(1024)} custom-call(s32[16384]{0:T(1024)} %reshape.51.idx_ref, f32[16384]{0:T(1024)} %reshape.53.val_ref), custom_call_target="tpu_custom_call" | custom-call | flops 4000000000 | bytes 270336 | tf_op jit(solution)/shard_map/route_lists/pallas_call | solution.py:69
  132.5 3.3 all-to-all-start.1
  136.5 3.9 all-to-all-done.1
  141.1 1.3 copy-done.1
  142.5 119.1 %forward_partial.1 = (f32[32768,128]{1,0:T(8,128)}, bf16[32,1024,512]{2,1,0:T(8,128)(2,1)}, s32[32]{0:T(128)}) custom-call(s32[33920]{0:T(1024)} %concatenate.9.tok_hbm, f32[33920]{0:T(1024)} %concatenate.10.g_hbm, bf16[8192,512]{1,0:T(8,128)(2,1)} %all-gather.5.cloned.1.call-done.x_hbm, bf16[8192,512]{1,0:T(8,128)(2,1)} %bitcast.30, ...), custom_call_target="tpu_custom_call" | custom-call | flops 38654705664 | bytes 75497472 | tf_op jit(solution)/shard_map/forward_partial/pallas_call | solution.py:291
  261.6 169.5 %backward_partial.1 = (f32[24576,128]{1,0:T(8,128)}, f32[8192,128]{1,0:T(8,128)}, bf16[32,1024,512]{2,1,0:T(8,128)(2,1)}, bf16[32,1024,768]{2,1,0:T(8,128)(2,1)}...) custom-call(s32[33920]{0:T(1024)} %concatenate.9.tok_hbm, ...), custom_call_target="tpu_custom_call" | custom-call | flops 64424509440 | bytes 150994944 | tf_op jit(solution)/shard_map/backward_partial/pallas_call | solution.py:368
  432.3 64.6 %reduce-scatter.8.cloned.1.call-done = f32[2048,128]{1,0:T(8,128)} async-done(((f32[8192,128]{1,0:T(8,128)}), f32[2048,128]{1,0:T(8,128)}) %reduce-scatter.8.cloned.1.call-update) | async-done | bytes 1048592 | tf_op jit(solution)/shard_map/reduce_scatter | solution.py:432
  496.9 1.3 convert_element_type.29
  498.5 1.5 collective-permute-start.5
  500.0 94.2 %reduce-scatter.6.cloned.1.call-done = f32[6144,128]{1,0:T(8,128)} async-done(((f32[24576,128]{1,0:T(8,128)}), f32[6144,128]{1,0:T(8,128)}) %reduce-scatter.6.cloned.1.call-update) | async-done | bytes 3145744 | tf_op jit(solution)/shard_map/reduce_scatter | solution.py:432
  594.2 2.0 convert_element_type.27
  596.3 2.4 convert_element_type.28
  598.7 1.5 collective-permute-start.4
  600.1 100.2 %weight_grads.2 = (bf16[32,512,768]{2,1,0:T(8,128)(2,1)}, bf16[32,512,768]{2,1,0:T(8,128)(2,1)}, bf16[32,768,512]{2,1,0:T(8,128)(2,1)}) custom-call(s32[32]{0:T(128)} %get-tuple-element.56.tiles, bf16[32,1024,512]{2,1,0:T(8,128)(2,1)} %get-tuple-element.57.x_ref, bf16[32,1024,512]{2,1,0:T(8,128)(2,1)} %get-tuple-element.53.d_ref, ...), custom_call_target="tpu_custom_call" | custom-call | flops 33822867456 | bytes 132120576 | tf_op jit(solution)/shard_map/weight_grads/pallas_call | solution.py:400
  700.3 17.1 %weight_grads.3 = (bf16[32,512,768]{2,1,0:T(8,128)(2,1)}, bf16[32,512,768]{2,1,0:T(8,128)(2,1)}, bf16[32,768,512]{2,1,0:T(8,128)(2,1)}) custom-call(s32[32]{0:T(128)} %get-tuple-element.56.tiles, bf16[32,1024,512]{2,1,0:T(8,128)(2,1)} %get-tuple-element.57.x_ref, ...), custom_call_target="tpu_custom_call", output_to_operand_aliasing={{0}: (6, {}), {1}: (7, {}), {2}: (8, {})} | custom-call | flops 4831838208 | bytes 18874368 | tf_op jit(solution)/shard_map/weight_grads/pallas_call | solution.py:400
  717.5 3.0 maximum_bitcast_fusion
  720.5 2.4 convert_element_type.25
  722.9 2.6 convert_element_type.26
  (33 shorter events, 8.6 us)
Async XLA Ops:
  7.2 133.9 %all-gather.9.cloned.1.call-start = ((), (), s32[]{:S(2)}) async-start(), calls=%async_computation.10 | async-start | bytes 10485760 | tf_op jit(solution)/shard_map/all_gather | solution.py:429
  7.9 133.2 %all-gather.5.cloned.1.call-start = ((), (), s32[]{:S(2)}) async-start(), calls=%async_computation.5 | async-start | bytes 10485760 | tf_op jit(solution)/shard_map/all_gather | solution.py:429
  7.9 5.9 collective-permute-start
  11.3 4.5 collective-permute-start.1
  15.8 56.8 %collective-permute-start.2 = (bf16[2048,512]{1,0:T(8,128)(2,1)}, bf16[2048,512]{1,0:T(8,128)(2,1)S(1)}, u32[]{:S(2)}, u32[]{:S(2)}) collective-permute-start(bf16[2048,512]{1,0:T(8,128)(2,1)} %bitcast.31), channel_id=1, source_target_pairs={{0,4},{4,0},{1,5},{5,1},{2,6},{6,2},{3,7},{7,3}} | collective-permute-start | bytes 6291464 | tf_op jit(solution)/shard_map/ppermute | solution.py:444
  72.6 1.3 copy-start
  73.9 67.2 %collective-permute-start.3 = (bf16[2048,512]{1,0:T(8,128)(2,1)}, bf16[2048,512]{1,0:T(8,128)(2,1)S(1)}, u32[]{:S(2)}, u32[]{:S(2)}) collective-permute-start(bf16[2048,512]{1,0:T(8,128)(2,1)} %bitcast.32), channel_id=1, source_target_pairs={{0,4},{4,0},{1,5},{5,1},{2,6},{6,2},{3,7},{7,3}} | collective-permute-start | bytes 6291464 | tf_op jit(solution)/shard_map/ppermute | solution.py:452
  75.0 57.5 %all-to-all-start = ((s32[4,1,8448]{2,1,0:T(1,128)}), s32[4,1,8448]{2,1,0:T(1,128)S(1)}, u32[]{:S(2)}, u32[]{:S(2)}) async-start(s32[4,1,8448]{2,1,0:T(1,128)} %bitcast.22), calls=%async_computation | async-start | bytes 270336 | tf_op jit(solution)/shard_map/all_to_all | solution.py:438
  132.5 8.0 %all-to-all-start.1 = ((f32[4,1,8448]{2,1,0:T(1,128)}), f32[4,1,8448]{2,1,0:T(1,128)S(1)}, u32[]{:S(2)}, u32[]{:S(2)}) async-start(f32[4,1,8448]{2,1,0:T(1,128)} %bitcast.23), calls=%async_computation.1 | async-start | bytes 270336 | tf_op jit(solution)/shard_map/all_to_all | solution.py:438
  135.8 125.8 %all-gather.7.cloned.1.call-start = ((), (), s32[]{:S(2)}) async-start(), calls=%async_computation.6 | async-start | bytes 10485760 | tf_op jit(solution)/shard_map/all_gather | solution.py:429
  141.1 1.3 copy-start.1
  142.4 354.5 %reduce-scatter.8.cloned.1.call-start = ((), (), s32[]{:S(2)}) async-start(), calls=%async_computation.9 | async-start | bytes 5242880 | tf_op jit(solution)/shard_map/reduce_scatter | solution.py:432
  431.1 163.1 %reduce-scatter.6.cloned.1.call-start = ((), (), s32[]{:S(2)}) async-start(), calls=%async_computation.8 | async-start | bytes 15728640 | tf_op jit(solution)/shard_map/reduce_scatter | solution.py:432
  431.7 288.8 %reduce-scatter.4.cloned.1.call-start = ((), (), s32[]{:S(2)}) async-start(), calls=%async_computation.7 | async-start | bytes 20971520 | tf_op jit(solution)/shard_map/reduce_scatter | solution.py:432
  498.5 218.9 %collective-permute-start.5 = (bf16[512,512]{1,0:T(8,128)(2,1)S(1)}, bf16[512,512]{1,0:T(8,128)(2,1)}, u32[]{:S(2)}, u32[]{:S(2)}) collective-permute-start(bf16[512,512]{1,0:T(8,128)(2,1)S(1)} %convert_element_type.30), channel_id=1, source_target_pairs={{4,0},{0,4},{5,1},{1,5},{6,2},{2,6},{7,3},{3,7}} | collective-permute-start | bytes 1572872 | tf_op jit(solution)/shard_map/ppermute | solution.py:466
  598.7 118.8 %collective-permute-start.4 = (bf16[1536,512]{1,0:T(8,128)(2,1)}, bf16[1536,512]{1,0:T(8,128)(2,1)}, u32[]{:S(2)}, u32[]{:S(2)}) collective-permute-start(bf16[1536,512]{1,0:T(8,128)(2,1)} %convert_element_type.28), channel_id=1, source_target_pairs={{4,0},{0,4},{5,1},{1,5},{6,2},{2,6},{7,3},{3,7}} | collective-permute-start | bytes 4718600 | tf_op jit(solution)/shard_map/ppermute | solution.py:465
Sparse Core Ops, SparseCore 0:
  9.5 58.2 all-gather.8
  74.0 55.9 all-gather.4
  142.6 54.9 all-gather.6
  431.2 65.6 reduce-scatter.7
  499.9 94.2 reduce-scatter.5
  596.6 119.4 reduce-scatter.3
